TPU v7x, 32 devices: a 4x4x1 block of a 4x4x8 slice. The times are simulated.
32 devices in a mesh: dp: 1 (over z), pz: 4 (over y), py: 8 (over x, core).
Axes of the slice: x: 4, y: 4, z: 1, core: 2. Of those that a mesh axis runs over, the one named last changes fastest.
The devices are a block of a 4x4x8 slice.
Arguments:
- rho_re: float32 [2, 256, 256, 256], P('dp', None, 'py', 'pz')
- rho_im: float32 [2, 256, 256, 256], P('dp', None, 'py', 'pz')
- g_re: float32 [256, 256, 256], P('py', 'pz')
- g_im: float32 [256, 256, 256], P('py', 'pz')
Outputs:
- output 1: float32 [2, 256, 256, 256], P('dp', None, 'py', 'pz')
- output 2: float32 [2, 256, 256, 256], P('dp', None, 'py', 'pz')
- output 3: float32 [2, 256, 256, 256], P('dp', 'py', 'pz')
- output 4: float32 [2, 256, 256, 256], P('dp', 'py', 'pz')
All inputs are finite; a program needn't handle non-finite values.
Results may differ from a plain program's by a relative error of at most 0.001.
Values sent between devices are 32-bit elements.
A program may use at most 768 MiB of HBM per device.

v0:
```python
import jax
import jax.numpy as jnp
from jax import lax
from jax.sharding import PartitionSpec as P


def regroup(volume, axis_name, split_dim, concat_dim):
    halves = jnp.stack([jnp.real(volume), jnp.imag(volume)])
    arrived = lax.all_to_all(halves, axis_name, split_dim + 1, concat_dim + 1, tiled=True)
    return lax.complex(arrived[0], arrived[1])


def solution(mesh):
    def local_solve(rho_re, rho_im, g_re, g_im):
        volume = jnp.fft.fft(lax.complex(rho_re, rho_im), axis=1, norm="ortho")
        volume = regroup(volume, "py", 1, 2)
        volume = jnp.fft.fft(volume, axis=2, norm="ortho")
        volume = regroup(volume, "pz", 2, 3)
        spectrum = jnp.fft.fft(volume, axis=3, norm="ortho") * lax.complex(g_re, g_im)
        volume = jnp.fft.ifft(spectrum, axis=3, norm="ortho")
        volume = regroup(volume, "pz", 3, 2)
        volume = jnp.fft.ifft(volume, axis=2, norm="ortho")
        volume = regroup(volume, "py", 2, 1)
        volume = jnp.fft.ifft(volume, axis=1, norm="ortho")
        return jnp.real(volume), jnp.imag(volume), jnp.real(spectrum), jnp.imag(spectrum)

    space_layout = P("dp", None, "py", "pz")
    wave_layout = P("dp", "py", "pz", None)
    green_layout = P("py", "pz", None)
    return jax.shard_map(local_solve, mesh=mesh,
                         in_specs=(space_layout, space_layout, green_layout, green_layout),
                         out_specs=(space_layout, space_layout, wave_layout, wave_layout),
                         check_vma=False)
```

profile of v0, /device:TPU:97, one launch (start us, length us, event | category | flops | bytes accessed | tf_op | source)
XLA Modules:
  0.0 1016.5 jit_solution(13083832111907479891)
XLA Ops:
  0.6 9.2 fusion.26
  24.3 16.2 %copy.42 = f32[2,2,256,32,64]{4,3,1,0,2:T(8,128)} copy(f32[2,2,256,32,64]{2,4,3,1,0:T(8,128)} %pad_maximum_fusion) | data formatting | bytes 16777216 | tf_op jit(solution)/shard_map/stack | solution.py:8
  40.5 15.6 %reshape.98 = f32[8,1,262144]{2,1,0:T(1,128)} reshape(f32[256,2,2,32,64]{4,3,2,1,0:T(8,128)} %bitcast.241) | data formatting | bytes 16777216
  56.1 101.1 %all_to_all.56 = f32[8,1,262144]{2,1,0:T(1,128)} all-to-all(f32[8,1,262144]{2,1,0:T(1,128)} %reshape.98), channel_id=1, replica_groups=mesh['dp'=1,'pz'=4,'py'=8] {'py'}, dimensions={0} | all-to-all | bytes 16777216 | tf_op jit(solution)/shard_map/all_to_all | solution.py:9
  157.8 26.2 %reduce.6 = f32[8,262144]{1,0:T(8,128)} reduce(f32[8,1,262144]{2,1,0:T(1,128)} %all_to_all.56, f32[]{:T(128)} %broadcast.228), dimensions={1}, to_apply=%all_to_all.40.reduce_sub_computation | reduce | bytes 16777220 | tf_op jit(solution)/shard_map/all_to_all | solution.py:9
  184.0 15.6 %reshape.99 = f32[256,2,2,32,64]{4,3,2,1,0:T(8,128)} reshape(f32[8,262144]{1,0:T(8,128)} %reduce.6) | data formatting | bytes 16777216
  199.7 6.9 copy.43
  206.6 6.8 fusion.171
  213.4 8.0 copy.44
  221.5 7.2 copy.45
  228.6 8.1 copy.46
  236.7 6.8 copy.47
  243.5 8.7 fusion.20
  266.2 16.2 %copy.48 = f32[2,2,32,256,64]{4,2,1,0,3:T(8,128)} copy(f32[2,2,32,256,64]{3,4,2,1,0:T(8,128)} %pad_maximum_fusion.1) | data formatting | bytes 16777216 | tf_op jit(solution)/shard_map/stack | solution.py:8
  282.5 14.5 %reshape.100 = f32[4,1,524288]{2,1,0:T(1,128)} reshape(f32[256,2,2,32,64]{4,3,2,1,0:T(8,128)} %bitcast.242) | data formatting | bytes 16777216
  302.7 93.3 %all-to-all-done.1 = f32[4,1,524288]{2,1,0:T(1,128)} async-done(((f32[4,1,524288]{2,1,0:T(1,128)}), f32[4,1,524288]{2,1,0:T(1,128)}, u32[]{:S(2)}, u32[]{:S(2)}) %all-to-all-start.1) | async-done | bytes 8388640 | tf_op jit(solution)/shard_map/all_to_all | solution.py:9
  396.0 28.2 %reduce.7 = f32[4,524288]{1,0:T(4,128)} reduce(f32[4,1,524288]{2,1,0:T(1,128)} %all-to-all-done.1, f32[]{:T(128)} %broadcast.228), dimensions={1}, to_apply=%all_to_all.43.reduce_sub_computation | reduce | bytes 16777220 | tf_op jit(solution)/shard_map/all_to_all | solution.py:9
  424.2 16.8 %reshape.101 = f32[256,2,2,32,64]{4,3,2,1,0:T(8,128)} reshape(f32[4,524288]{1,0:T(4,128)} %reduce.7) | data formatting | bytes 16777216
  441.0 19.3 %copy.73 = f32[2,2,32,4,64,64]{5,3,4,2,1,0:T(4,128)S(1)} copy(f32[2,2,32,4,64,64]{5,2,1,0,4,3:T(8,128)} %bitcast.250) | data formatting | bytes 16777216 | tf_op jit(solution)/shard_map/all_to_all | solution.py:9
  460.3 6.2 fusion.170
  466.5 8.6 squeeze.27
  475.1 8.6 squeeze.26
  483.6 8.8 fusion.32
  512.1 6.4 fusion.17
  522.4 16.2 %copy.50 = f32[2,2,32,64,256]{3,2,1,0,4:T(8,128)} copy(f32[2,2,32,64,256]{4,3,2,1,0:T(8,128)} %pad_maximum_fusion.2) | data formatting | bytes 16777216 | tf_op jit(solution)/shard_map/stack | solution.py:8
  538.6 14.3 %reshape.102 = f32[4,1,524288]{2,1,0:T(1,128)} reshape(f32[256,2,2,32,64]{4,3,2,1,0:T(8,128)} %bitcast.243) | data formatting | bytes 16777216
  552.9 99.2 %all_to_all.57 = f32[4,1,524288]{2,1,0:T(1,128)} all-to-all(f32[4,1,524288]{2,1,0:T(1,128)} %reshape.102), channel_id=1, replica_groups=mesh['dp'=1,'pz'=4,'py'=8] {'pz'}, dimensions={0} | all-to-all | bytes 16777216 | tf_op jit(solution)/shard_map/all_to_all | solution.py:9
  652.1 28.2 %reduce.8 = f32[4,524288]{1,0:T(4,128)} reduce(f32[4,1,524288]{2,1,0:T(1,128)} %all_to_all.57, f32[]{:T(128)} %broadcast.228), dimensions={1}, to_apply=%all_to_all.46.reduce_sub_computation | reduce | bytes 16777220 | tf_op jit(solution)/shard_map/all_to_all | solution.py:9
  680.3 16.8 %reshape.103 = f32[256,2,2,32,64]{4,3,2,1,0:T(8,128)} reshape(f32[4,524288]{1,0:T(4,128)} %reduce.8) | data formatting | bytes 16777216
  697.1 19.3 %copy.72 = f32[2,2,32,64,4,64]{3,4,5,2,1,0:T(4,128)S(1)} copy(f32[2,2,32,64,4,64]{3,2,1,0,5,4:T(8,128)} %bitcast.251) | data formatting | bytes 16777216 | tf_op jit(solution)/shard_map/all_to_all | solution.py:9
  716.4 6.2 fusion.169
  722.6 8.6 squeeze.28
  731.1 8.6 squeeze.29
  739.7 9.0 fusion.12
  753.5 6.2 fusion.9
  763.5 16.6 %copy.52 = f32[2,2,32,256,64]{4,2,1,0,3:T(8,128)} copy(f32[2,2,32,256,64]{3,4,2,1,0:T(8,128)} %pad_maximum_fusion.3) | data formatting | bytes 16777216 | tf_op jit(solution)/shard_map/stack | solution.py:8
  780.1 15.4 %reshape.104 = f32[8,1,262144]{2,1,0:T(1,128)} reshape(f32[256,2,2,32,64]{4,3,2,1,0:T(8,128)} %bitcast.244) | data formatting | bytes 16777216
  795.5 101.8 %all_to_all.58 = f32[8,1,262144]{2,1,0:T(1,128)} all-to-all(f32[8,1,262144]{2,1,0:T(1,128)} %reshape.104), channel_id=1, replica_groups=mesh['dp'=1,'pz'=4,'py'=8] {'py'}, dimensions={0} | all-to-all | bytes 16777216 | tf_op jit(solution)/shard_map/all_to_all | solution.py:9
  897.3 26.2 %reduce.9 = f32[8,262144]{1,0:T(8,128)} reduce(f32[8,1,262144]{2,1,0:T(1,128)} %all_to_all.58, f32[]{:T(128)} %broadcast.228), dimensions={1}, to_apply=%all_to_all.49.reduce_sub_computation | reduce | bytes 16777220 | tf_op jit(solution)/shard_map/all_to_all | solution.py:9
  923.5 15.6 %reshape.105 = f32[256,2,2,32,64]{4,3,2,1,0:T(8,128)} reshape(f32[8,262144]{1,0:T(8,128)} %reduce.9) | data formatting | bytes 16777216
  939.2 15.4 %copy.53 = f32[2,2,32,256,64]{4,3,2,1,0:T(8,128)S(1)} copy(f32[2,2,32,256,64]{4,2,1,0,3:T(8,128)} %bitcast.252) | data formatting | bytes 16777216 | tf_op jit(solution)/shard_map/all_to_all | solution.py:9
  954.6 6.8 fusion.168
  961.4 8.0 copy.54
  969.4 7.8 copy.55
  977.2 8.0 copy.56
  985.3 7.8 copy.57
  993.1 9.0 fusion.4
  1006.9 9.4 fusion
  (44 shorter events, 71.7 us)
Async XLA Ops:
  0.6 9.2 copy-start.10
  9.9 4.9 copy-start.11
  243.5 8.7 copy-start.1
  252.2 4.7 copy-start.2
  297.0 99.0 %all-to-all-start.1 = ((f32[4,1,524288]{2,1,0:T(1,128)}), f32[4,1,524288]{2,1,0:T(1,128)}, u32[]{:S(2)}, u32[]{:S(2)}) async-start(f32[4,1,524288]{2,1,0:T(1,128)} %reshape.100), calls=%async_computation.1 | async-start | bytes 16777216 | tf_op jit(solution)/shard_map/all_to_all | solution.py:9
  483.6 8.8 copy-start.4
  492.4 4.5 copy-start.3
  492.4 4.5 copy-start.12
  492.4 4.5 copy-start.13
  502.7 4.8 copy-start
  502.7 9.4 copy-start.7
  739.7 9.0 copy-start.5
  748.7 4.9 copy-start.9
  993.1 9.0 copy-start.6
  1002.1 4.9 copy-start.8
where the time goes:
time: 1020 us
  local copies, waits for them, and re-layouts  373 us (37%)
  blocking collectives  302 us (30%)
  other arithmetic  124 us (12%)
  matrix products  117 us (11%)
  waiting for transfers between devices  93.3 us (9%)
    all_to_all x3, blocking collectives, regroup(): lax.all_to_all(halves, axis_name, split_dim + 1, concat_dim + 1, tiled=True)  302 us
    unnamed x36, local copies, waits for them, and re-layouts  125 us
    all_to_all x4, other arithmetic, regroup(): lax.all_to_all(halves, axis_name, split_dim + 1, concat_dim + 1, tiled=True)  109 us
    all_to_all x1, waiting for transfers between devices, regroup(): lax.all_to_all(halves, axis_name, split_dim + 1, concat_dim + 1, tiled=True)  93.3 us
    another operation x4, local copies, waits for them, and re-layouts, regroup(): halves = jnp.stack([jnp.real(volume), jnp.imag(volume)])  65.3 us
    squeeze x8, local copies, waits for them, and re-layouts, regroup(): return lax.complex(arrived[0], arrived[1])  63.7 us
    all_to_all x5, local copies, waits for them, and re-layouts, regroup(): lax.all_to_all(halves, axis_name, split_dim + 1, concat_dim + 1, tiled=True)  61.5 us
    slice x8, local copies, waits for them, and re-layouts, regroup(): return lax.complex(arrived[0], arrived[1])  58.1 us
  transfers between devices with their start and end apart: 1, of which 1 were waited for; matrix products, arithmetic and copies ran while one was open for 0% of the time, Pallas kernels for 0%

commit v1 on v0

v1 whole, which is shorter than its diff:
```python
import functools

import jax
import jax.numpy as jnp
import numpy as np
from jax import lax
from jax.experimental import pallas as pl
from jax.experimental.pallas import tpu as pltpu
from jax.sharding import PartitionSpec as P

MESH = pl.DeviceIdType.MESH
HALF_X_CHUNKS = 4
LANES = 128


def real_form(matrix):
    return np.block([[matrix.real, -matrix.imag], [matrix.imag, matrix.real]])


def dft_tables(n, ny, nz):
    half = n // 2
    scale = 1.0 / np.sqrt(n)
    low, full = np.arange(half), np.arange(n)
    dft = lambda k, j, sign: scale * np.exp(sign * 2j * np.pi * ((k[:, None] * j[None, :]) % n) / n)
    per = n // ny // HALF_X_CHUNKS // 2
    order = np.arange(half).reshape(ny, HALF_X_CHUNKS, per).transpose(1, 0, 2)
    rows = np.stack([order, order + half], axis=2).reshape(-1)
    wx = np.stack([real_form(dft(2 * low + p, low, -1))[rows] for p in range(2)])
    wxi = np.stack([real_form(dft(low, 2 * low + p, 1))[:, rows].T for p in range(2)])
    wy = np.stack([real_form(dft(2 * low + p, low, -1)) for p in range(2)])
    wyi = np.stack([real_form(dft(low, 2 * low + p, 1)) for p in range(2)])
    lz = n // nz
    zrows = np.arange(n).reshape(nz, lz)
    zrows = np.stack([zrows, zrows + n], axis=1).reshape(-1)
    wz = real_form(dft(full, full, -1)).T[zrows]
    wzi = real_form(dft(full, full, 1)).T[:, zrows]
    return [np.asarray(w, np.float32) for w in (wx, wy, wz, wzi, wyi, wxi)]


def dot(a, b, dims=((1,), (0,))):
    return lax.dot_general(a, b, (dims, ((), ())), precision=lax.Precision.HIGHEST,
                           preferred_element_type=jnp.float32)


def kernel(ny, nz, n, nf,
           rho_re, rho_im, g_re, g_im, wx_h, wy_h, wz_h, wzi_h, wyi_h, wxi_h,
           phi_re, phi_im, hat_re, hat_im,
           abuf, bbuf, cbuf, dbuf, ebuf, even, stage, gbuf, hbuf, wx, wy, wz, wzi, wyi, wxi,
           xs, xr, ys, yr, yis, yir, xis, xir, w_sem, in_sem, g_sem, h_sem):
    py, pz = lax.axis_index("py"), lax.axis_index("pz")
    half = n // 2
    yl, zl = n // ny, n // nz
    kc = n // ny // HALF_X_CHUNKS // 2
    nj = 2 * HALF_X_CHUNKS
    xrow, yrow = yl * 2 * kc, 2 * kc * zl
    crow = ny * xrow
    rho, phi, gg, hat = (rho_re, rho_im), (phi_re, phi_im), (g_re, g_im), (hat_re, hat_im)
    x_offsets = (4, 3, 5, 2, 6, 1, 7) if ny == 8 else tuple(range(1, ny))
    y_offsets = (2, 1, 3) if nz == 4 else tuple(range(1, nz))

    barrier = pltpu.get_barrier_semaphore()
    for o in range(1, ny):
        pl.semaphore_signal(barrier, inc=1, device_id={"py": lax.rem(py + o, ny)}, device_id_type=MESH)
    for o in range(1, nz):
        pl.semaphore_signal(barrier, inc=1, device_id={"pz": lax.rem(pz + o, nz)}, device_id_type=MESH)

    tables = [pltpu.make_async_copy(h, v, w_sem.at[i]) for i, (h, v) in enumerate(
        ((wx_h, wx), (wy_h, wy), (wz_h, wz), (wzi_h, wzi), (wyi_h, wyi), (wxi_h, wxi)))]

    def rho_copy(c, pair, slot):
        return pltpu.make_async_copy(rho[c].at[:, pl.ds(2 * pair, 2)], stage.at[slot, c], in_sem.at[slot, c])

    def phi_copy(c, pair, slot):
        return pltpu.make_async_copy(stage.at[slot, c], phi[c].at[:, pl.ds(2 * pair, 2)], in_sem.at[slot, c])

    def g_copy(c, j):
        p, jj, slot = j // HALF_X_CHUNKS, lax.rem(j, HALF_X_CHUNKS), lax.rem(j, 2)
        return pltpu.make_async_copy(gg[c].at[pl.ds(kc * jj, kc), p], gbuf.at[slot, c], g_sem.at[slot, c])

    def hat_copy(c, f, j):
        p, jj, slot = j // HALF_X_CHUNKS, lax.rem(j, HALF_X_CHUNKS), lax.rem(j, 2)
        return pltpu.make_async_copy(hbuf.at[slot, c, f], hat[c].at[f, pl.ds(kc * jj, kc), p], h_sem.at[slot, c, f])

    def x_copy(src, dst, ss, rs, j, o):
        to = lax.rem(py + o, ny)
        return pltpu.make_async_remote_copy(
            src.at[pl.ds(pl.multiple_of(j * crow + to * xrow, 8), xrow)],
            dst.at[pl.ds(pl.multiple_of(j * crow + py * xrow, 8), xrow)],
            ss.at[j, o - 1], rs.at[j, o - 1], device_id={"py": to}, device_id_type=MESH)

    def y_copy(src, dst, ss, rs, j, o):
        to = lax.rem(pz + o, nz)
        return pltpu.make_async_remote_copy(
            src.at[pl.ds(pl.multiple_of(j * crow + to * yrow, 8), yrow)],
            dst.at[pl.ds(pl.multiple_of(j * crow + pz * yrow, 8), yrow)],
            ss.at[j, o - 1], rs.at[j, o - 1], device_id={"pz": to}, device_id_type=MESH)

    def own(src, dst, j, mine, rows):
        at = pl.ds(pl.multiple_of(j * crow + mine * rows, 8), rows)
        dst[at, :] = src[at, :]

    xf = functools.partial(x_copy, abuf, bbuf, xs, xr)
    yf = functools.partial(y_copy, abuf, cbuf, ys, yr)
    yi = functools.partial(y_copy, cbuf, dbuf, yis, yir)
    xi = functools.partial(x_copy, bbuf, ebuf, xis, xir)

    def x_forward(p):
        for c in range(2):
            rho_copy(c, 0, 0).start()

        def body(pair, carry):
            slot = lax.rem(pair, 2)
            for c in range(2):
                rho_copy(c, pair, slot).wait()

            @pl.when(pair + 1 < yl // 2)
            def _():
                for c in range(2):
                    rho_copy(c, pair + 1, 1 - slot).start()

            folded = []
            for c in range(2):
                lines = stage[slot, c]
                first, second = lines[..., :half], lines[..., half:]
                both = first - second if p else first + second
                folded.append(jnp.swapaxes(both, 0, 1).reshape(2 * nf * zl, half))
            out = dot(wx[p], jnp.concatenate(folded, axis=1), ((1,), (1,)))
            for jj in range(HALF_X_CHUNKS):
                for to in range(ny):
                    r = (jj * ny + to) * 2 * kc
                    for y in range(2):
                        at = (p * HALF_X_CHUNKS + jj) * crow + to * xrow + (2 * pair + y) * 2 * kc
                        abuf[pl.ds(pl.multiple_of(at, 8), 2 * kc), :] = out[r:r + 2 * kc, y * LANES:(y + 1) * LANES]
            return carry

        lax.fori_loop(0, yl // 2, body, 0)

    def x_send(p):
        for jj in range(HALF_X_CHUNKS):
            j = p * HALF_X_CHUNKS + jj
            for o in x_offsets:
                xf(j, o).start()

    def y_forward(j):
        own(abuf, bbuf, j, py, xrow)
        base = j * crow
        for i0 in range(0, kc, 2):
            parts = []
            for c in range(2):
                parts.append(jnp.concatenate(
                    [bbuf[pl.ds(base + c * kc + i, n, stride=2 * kc), :] for i in (i0, i0 + 1)], axis=1))
            for p in range(2):
                folded = jnp.concatenate([v[:half] - v[half:] if p else v[:half] + v[half:] for v in parts], axis=0)
                out = dot(wy[p], folded)
                for c in range(2):
                    for to in range(nz):
                        for k in range(2):
                            at = base + to * yrow + (c * kc + i0 + k) * zl + p
                            abuf[pl.ds(at, zl // 2, stride=2), :] = out[
                                c * half + to * zl // 2:c * half + (to + 1) * zl // 2, k * LANES:(k + 1) * LANES]

    def z_solve(j):
        own(abuf, cbuf, j, pz, yrow)
        base, slot = j * crow, lax.rem(j, 2)
        rows = kc * zl
        left = lax.broadcasted_iota(jnp.int32, (rows, LANES), 1) < zl
        swap = lambda v: pltpu.roll(v, zl, 1)
        lines = ([], [])
        for b in range(nz):
            at = base + b * yrow
            re = cbuf[pl.ds(pl.multiple_of(at, 8), rows), :]
            im = cbuf[pl.ds(pl.multiple_of(at + rows, 8), rows), :]
            lines[0].append(jnp.where(left, re, swap(im)))
            lines[1].append(jnp.where(left, swap(re), im))
        gr = gbuf[slot, 0].reshape(rows, n)
        gi = gbuf[slot, 1].reshape(rows, n)
        back = []
        for f in range(nf):
            spec = dot(jnp.concatenate(lines[f], axis=1), wz[...])
            sr, si = spec[:, :n], spec[:, n:]
            hr, hi = sr * gr - si * gi, sr * gi + si * gr
            hbuf[slot, 0, f] = hr.reshape(kc, zl, n)
            hbuf[slot, 1, f] = hi.reshape(kc, zl, n)
            back.append(dot(jnp.concatenate([hr, hi], axis=1), wzi[...]))
        for b in range(nz):
            first, second = (v[:, b * LANES:(b + 1) * LANES] for v in back)
            at = base + b * yrow
            cbuf[pl.ds(pl.multiple_of(at, 8), rows), :] = jnp.where(left, first, swap(second))
            cbuf[pl.ds(pl.multiple_of(at + rows, 8), rows), :] = jnp.where(left, swap(first), second)

    def y_inverse(j):
        own(cbuf, dbuf, j, pz, yrow)
        base = j * crow
        for i0 in range(0, kc, 2):
            halves = []
            for p in range(2):
                lines = []
                for k in range(2):
                    lines.append(jnp.concatenate(
                        [dbuf[pl.ds(base + src * yrow + (c * kc + i0 + k) * zl + p, zl // 2, stride=2), :]
                         for c in range(2) for src in range(nz)], axis=0))
                halves.append(dot(wyi[p], jnp.concatenate(lines, axis=1)))
            for s, out in enumerate((halves[0] + halves[1], halves[0] - halves[1])):
                for c in range(2):
                    for k in range(2):
                        at = base + s * (ny // 2) * xrow + c * kc + i0 + k
                        bbuf[pl.ds(at, half, stride=2 * kc), :] = out[
                            c * half:(c + 1) * half, k * LANES:(k + 1) * LANES]

    def x_gather(p, pair):
        lines = []
        for y in range(2):
            lines.append(jnp.concatenate(
                [ebuf[pl.ds(pl.multiple_of((p * HALF_X_CHUNKS + jj) * crow + src * xrow + (2 * pair + y) * 2 * kc, 8),
                            2 * kc), :]
                 for jj in range(HALF_X_CHUNKS) for src in range(ny)], axis=0))
        return dot(jnp.concatenate(lines, axis=1), wxi[p], ((0,), (0,)))

    for table in tables:
        table.start()
    for c in range(2):
        g_copy(c, 0).start()
        g_copy(c, 1).start()
    tables[0].wait()
    x_forward(0)
    pl.semaphore_wait(barrier, ny + nz - 2)
    x_send(0)
    x_forward(1)
    x_send(1)
    for table in tables[1:]:
        table.wait()

    def step(t, carry):
        @pl.when(t < nj)
        def _():
            for o in x_offsets:
                xf(t, o).wait()
            y_forward(t)
            for o in y_offsets:
                yf(t, o).start()

        @pl.when((t >= 1) & (t < nj + 1))
        def _():
            j = t - 1
            for o in y_offsets:
                yf(j, o).wait()
            for c in range(2):
                g_copy(c, j).wait()

            @pl.when(j >= 2)
            def _():
                for c in range(2):
                    for f in range(nf):
                        hat_copy(c, f, j - 2).wait()

            z_solve(j)
            for o in y_offsets:
                yi(j, o).start()
            for c in range(2):
                for f in range(nf):
                    hat_copy(c, f, j).start()

            @pl.when(j + 2 < nj)
            def _():
                for c in range(2):
                    g_copy(c, j + 2).start()

        @pl.when(t >= 2)
        def _():
            j = t - 2
            for o in y_offsets:
                yi(j, o).wait()
            y_inverse(j)
            for o in x_offsets:
                xi(j, o).start()
            own(bbuf, ebuf, j, py, xrow)

        @pl.when(t == nj)
        def _():
            for jj in range(HALF_X_CHUNKS):
                for o in x_offsets:
                    xi(jj, o).wait()

            def body(pair, c):
                even[pair] = x_gather(0, pair)
                return c

            lax.fori_loop(0, yl // 2, body, 0)

        return carry

    lax.fori_loop(0, nj + 2, step, 0)
    for jj in range(HALF_X_CHUNKS, nj):
        for o in x_offsets:
            xi(jj, o).wait()

    def finish(pair, carry):
        slot = lax.rem(pair, 2)

        @pl.when(pair >= 2)
        def _():
            for c in range(2):
                phi_copy(c, pair - 2, slot).wait()

        e, o = even[pair], x_gather(1, pair)
        for c in range(2):
            er, orr = e[:, c * half:(c + 1) * half], o[:, c * half:(c + 1) * half]
            out = jnp.concatenate([er + orr, er - orr], axis=1).reshape(2, nf, zl, n)
            stage[slot, c] = jnp.swapaxes(out, 0, 1)
            phi_copy(c, pair, slot).start()
        return carry

    lax.fori_loop(0, yl // 2, finish, 0)
    for pair in (yl // 2 - 2, yl // 2 - 1):
        for c in range(2):
            phi_copy(c, pair, pair % 2).wait()
    for j in (nj - 2, nj - 1):
        for c in range(2):
            for f in range(nf):
                hat_copy(c, f, j).wait()


def solution(mesh):
    ny, nz = mesh.shape["py"], mesh.shape["pz"]

    def local_solve(rho_re, rho_im, g_re, g_im):
        nf, n, yl, zl = rho_re.shape
        kl, ml = g_re.shape[:2]
        kc = kl // HALF_X_CHUNKS // 2
        nj = 2 * HALF_X_CHUNKS
        rows = nj * ny * yl * 2 * kc
        tables = [jnp.asarray(w) for w in dft_tables(n, ny, nz)]
        space = jax.ShapeDtypeStruct((nf, yl, zl, n), jnp.float32)
        wave = jax.ShapeDtypeStruct((nf, kl // 2, 2, ml, n), jnp.float32)
        dma = pltpu.SemaphoreType.DMA
        buf = pltpu.VMEM((rows, LANES), jnp.float32)
        outs = pl.pallas_call(
            functools.partial(kernel, ny, nz, n, nf),
            out_shape=(space, space, wave, wave),
            in_specs=[pl.BlockSpec(memory_space=pl.ANY)] * 10,
            out_specs=[pl.BlockSpec(memory_space=pl.ANY)] * 4,
            scratch_shapes=[
                buf, buf, buf, buf, buf,
                pltpu.VMEM((yl // 2, 2 * nf * zl, n), jnp.float32),
                pltpu.VMEM((2, 2, nf, 2, zl, n), jnp.float32),
                pltpu.VMEM((2, 2, kc, ml, n), jnp.float32),
                pltpu.VMEM((2, 2, nf, kc, ml, n), jnp.float32),
                *[pltpu.VMEM(t.shape, jnp.float32) for t in tables],
                dma((nj, ny - 1)), dma((nj, ny - 1)), dma((nj, nz - 1)), dma((nj, nz - 1)),
                dma((nj, nz - 1)), dma((nj, nz - 1)), dma((nj, ny - 1)), dma((nj, ny - 1)),
                dma((len(tables),)), dma((2, 2)), dma((2, 2)), dma((2, 2, nf)),
            ],
            compiler_params=pltpu.CompilerParams(
                collective_id=0, has_side_effects=True, vmem_limit_bytes=67043328),
            name="spectral",
        )(jnp.transpose(rho_re, (0, 2, 3, 1)), jnp.transpose(rho_im, (0, 2, 3, 1)),
          g_re.reshape(kl // 2, 2, ml, n), g_im.reshape(kl // 2, 2, ml, n), *tables)
        phi = [jnp.transpose(v, (0, 3, 1, 2)) for v in outs[:2]]
        return (*phi, *(v.reshape(nf, kl, ml, n) for v in outs[2:]))

    space_layout = P("dp", None, "py", "pz")
    wave_layout = P("dp", "py", "pz", None)
    green_layout = P("py", "pz", None)
    return jax.shard_map(local_solve, mesh=mesh,
                         in_specs=(space_layout, space_layout, green_layout, green_layout),
                         out_specs=(space_layout, space_layout, wave_layout, wave_layout),
                         check_vma=False)
```

time: 1020 us -> 268 us (0.26)
  local copies, waits for them, and re-layouts: 373 us -> 14.3 us
  blocking collectives: 302 us -> 0 us
  Pallas kernels: 0 us -> 253 us
  other arithmetic: 124 us -> 0 us
  matrix products: 117 us -> 0 us
  waiting for transfers between devices: 93.3 us -> 0 us
    all_to_all x3 -> x0, blocking collectives: 302 us -> none  [regroup(): lax.all_to_all(halves, axis_name, split_dim + 1, concat_dim + 1, tiled=True)]
    pallas_call x0 -> x1, Pallas kernels: none -> 253 us  [local_solve(): pl.pallas_call(functools.partial(kernel, ny, nz, n, nf), out_shape=(space...]
    another operation x18 -> x0, matrix products: 117 us -> none  [the longest x3 23.1 us: local_solve(): volume = jnp.fft.ifft(volume, axis=1, norm='ortho')]
    unnamed x36 -> x10, local copies, waits for them, and re-layouts: 125 us -> 14.3 us
    all_to_all x4 -> x0, other arithmetic: 109 us -> none  [regroup(): lax.all_to_all(halves, axis_name, split_dim + 1, concat_dim + 1, tiled=True)]
    all_to_all x1 -> x0, waiting for transfers between devices: 93.3 us -> none  [regroup(): lax.all_to_all(halves, axis_name, split_dim + 1, concat_dim + 1, tiled=True)]
    another operation x4 -> x0, local copies, waits for them, and re-layouts: 65.3 us -> none  [regroup(): halves = jnp.stack([jnp.real(volume), jnp.imag(volume)])]
    squeeze x8 -> x0, local copies, waits for them, and re-layouts: 63.7 us -> none  [regroup(): return lax.complex(arrived[0], arrived[1])]
  transfers between devices with their start and end apart: 1 -> 0, of which waited for: 1 -> 0; matrix products, arithmetic and copies ran while one was open for 0% -> 0% of each run, Pallas kernels for 0% -> 0%
where the time goes in v1:
time: 268 us; the launch traced here: 267 us
  Pallas kernels  253 us (94%)
  local copies, waits for them, and re-layouts  14.3 us (5%)
    pallas_call x1, Pallas kernels, local_solve(): pl.pallas_call(functools.partial(kernel, ny, nz, n, nf), out_shape=(space...  253 us
    unnamed x10, local copies, waits for them, and re-layouts  14.3 us

profile of v1, /device:TPU:97, one launch (start us, length us, event | category | flops | bytes accessed | tf_op | source)
XLA Modules:
  0.0 267.5 jit_solution(1371921759975293276)
XLA Ops:
  0.6 252.5 %spectral.1 = (f32[2,32,64,256]{3,2,1,0:T(8,128)}, f32[2,32,64,256]{3,2,1,0:T(8,128)}, f32[2,16,2,64,256]{4,3,2,1,0:T(8,128)}, f32[2,16,2,64,256]{4,3,2,1,0:T(8,128)}) custom-call(f32[2,32,64,256]{3,2,1,0:T(8,128)} %bitcast.12, f32[2,32,64,256]{3,2,1,0:T(8,128)} %bitcast.13, f32[16,2,64,256]{3,2,1,0:T(8,128)} %bitcast.14, f32[16,2,64,256]{3,2,1,0:T(8,128)} %bitcast.15, ...), custom_call_target="tpu_custom_call" | custom-call | tf_op jit(solution)/shard_map/spectral/pallas_call | solution.py:337
  253.2 0.0 copy-start.2
  253.2 4.8 %copy.18 = f32[2,256,32,64]{1,3,2,0:T(8,128)} copy(f32[2,256,32,64]{1,3,2,0:T(8,128)} %bitcast.11) | data formatting | bytes 8388608
  258.0 0.0 copy-done.2
  258.0 0.0 copy-start.1
  258.0 2.1 copy.19
  260.2 1.6 copy-done.1
  261.7 0.0 copy-start
  261.7 2.1 copy.20
  263.9 1.6 copy-done
  265.4 2.0 copy.21
Async XLA Ops:
  253.2 4.9 %copy-start.2 = (f32[2,32,64,256]{3,2,1,0:T(8,128)S(1)}, f32[2,32,64,256]{3,2,1,0:T(8,128)}, u32[]{:S(2)}) copy-start(f32[2,32,64,256]{3,2,1,0:T(8,128)} %get-tuple-element.9) | copy-start | bytes 12582916
  258.0 3.7 %copy-start.1 = (f32[2,16,2,64,256]{4,3,2,1,0:T(8,128)S(1)}, f32[2,16,2,64,256]{4,3,2,1,0:T(8,128)}, u32[]{:S(2)}) copy-start(f32[2,16,2,64,256]{4,3,2,1,0:T(8,128)} %get-tuple-element.10) | copy-start | bytes 12582916
  261.7 3.7 %copy-start = (f32[2,16,2,64,256]{4,3,2,1,0:T(8,128)S(1)}, f32[2,16,2,64,256]{4,3,2,1,0:T(8,128)}, u32[]{:S(2)}) copy-start(f32[2,16,2,64,256]{4,3,2,1,0:T(8,128)} %get-tuple-element.11) | copy-start | bytes 12582916

commit v2 on v1

v2 whole, which is shorter than its diff:
```python
import functools

import jax
import jax.numpy as jnp
import numpy as np
from jax import lax
from jax.experimental import pallas as pl
from jax.experimental.pallas import tpu as pltpu
from jax.sharding import PartitionSpec as P

MESH = pl.DeviceIdType.MESH
HALF_X_CHUNKS = 8
SLOTS = 4
LANES = 128
INNER_VMEM = 42 << 20


def real_form(matrix):
    return np.block([[matrix.real, -matrix.imag], [matrix.imag, matrix.real]])


def dft_tables(n, ny, nz):
    half = n // 2
    scale = 1.0 / np.sqrt(n)
    low, full = np.arange(half), np.arange(n)
    dft = lambda k, j, sign: scale * np.exp(sign * 2j * np.pi * ((k[:, None] * j[None, :]) % n) / n)
    per = n // ny // HALF_X_CHUNKS // 2
    order = np.arange(half).reshape(ny, HALF_X_CHUNKS, per).transpose(1, 0, 2)
    rows = np.stack([order, order + half], axis=2).reshape(-1)
    wx = np.stack([real_form(dft(2 * low + p, low, -1))[rows] for p in range(2)])
    wxi = np.stack([real_form(dft(low, 2 * low + p, 1))[:, rows].T for p in range(2)])
    wy = np.stack([real_form(dft(2 * low + p, low, -1)) for p in range(2)])
    wyi = np.stack([real_form(dft(low, 2 * low + p, 1)) for p in range(2)])
    lz = n // nz
    zrows = np.arange(n).reshape(nz, lz)
    zrows = np.stack([zrows, zrows + n], axis=1).reshape(-1)
    wz = real_form(dft(full, full, -1)).T[zrows]
    wzi = real_form(dft(full, full, 1)).T[:, zrows]
    return [np.asarray(w, np.float32) for w in (wx, wy, wz, wzi, wyi, wxi)]


def dot(a, b, dims=((1,), (0,))):
    return lax.dot_general(a, b, (dims, ((), ())), precision=lax.Precision.HIGHEST,
                           preferred_element_type=jnp.float32)


def swap_rows(first, second):
    a, b = first.reshape(-1, 8, LANES), second.reshape(-1, 8, LANES)
    upper = lax.broadcasted_iota(jnp.int32, a.shape, 1) < 4
    return jnp.where(upper, a, pltpu.roll(b, 4, 1)), jnp.where(upper, pltpu.roll(a, 4, 1), b)


def kernel(ny, nz, n, nf,
           rho_re, rho_im, g_re, g_im, wx_h, wy_h, wz_h, wzi_h, wyi_h, wxi_h,
           ebuf, even, hat_re, hat_im,
           abuf, bbuf, cbuf, dbuf, stage, gbuf, wx, wy, wz, wzi, wyi, wxi,
           xs, xr, ys, yr, yis, yir, xis, xir, w_sem, in_sem, g_sem):
    py, pz = lax.axis_index("py"), lax.axis_index("pz")
    half = n // 2
    yl, zl = n // ny, n // nz
    kc = n // ny // HALF_X_CHUNKS // 2
    nj = 2 * HALF_X_CHUNKS
    xrow, yrow = yl * 2 * kc, 2 * kc * zl
    crow = ny * xrow
    pairs = yl // 2
    quarter = pairs // 4
    rho, gg, hat = (rho_re, rho_im), (g_re, g_im), (hat_re, hat_im)
    x_offsets = (4, 3, 5, 2, 6, 1, 7) if ny == 8 else tuple(range(1, ny))
    y_offsets = (2, 1, 3) if nz == 4 else tuple(range(1, nz))

    barrier = pltpu.get_barrier_semaphore()
    for o in range(1, ny):
        pl.semaphore_signal(barrier, inc=1, device_id={"py": lax.rem(py + o, ny)}, device_id_type=MESH)
    for o in range(1, nz):
        pl.semaphore_signal(barrier, inc=1, device_id={"pz": lax.rem(pz + o, nz)}, device_id_type=MESH)

    tables = [pltpu.make_async_copy(h, v, w_sem.at[i]) for i, (h, v) in enumerate(
        ((wx_h, wx), (wy_h, wy), (wz_h, wz), (wzi_h, wzi), (wyi_h, wyi), (wxi_h, wxi)))]

    def rho_copy(c, pair):
        slot = lax.rem(pair, SLOTS)
        return pltpu.make_async_copy(rho[c].at[:, pl.ds(2 * pair, 2)], stage.at[slot, c], in_sem.at[slot, c])

    def g_copy(c, j):
        p, jj, slot = j // HALF_X_CHUNKS, lax.rem(j, HALF_X_CHUNKS), lax.rem(j, 2)
        return pltpu.make_async_copy(gg[c].at[pl.ds(kc * jj, kc), p], gbuf.at[slot, c], g_sem.at[slot, c])

    def x_copy(src, dst, ss, rs, j, o, first=0, count=None):
        to = lax.rem(py + o, ny)
        rows = xrow if count is None else count
        return pltpu.make_async_remote_copy(
            src.at[pl.ds(pl.multiple_of(j * crow + to * xrow + first, 8), rows)],
            dst.at[pl.ds(pl.multiple_of(j * crow + py * xrow + first, 8), rows)],
            ss.at[j], rs.at[j], device_id={"py": to}, device_id_type=MESH)

    def y_copy(src, dst, ss, rs, j, o):
        to = lax.rem(pz + o, nz)
        return pltpu.make_async_remote_copy(
            src.at[pl.ds(pl.multiple_of(j * crow + to * yrow, 8), yrow)],
            dst.at[pl.ds(pl.multiple_of(j * crow + pz * yrow, 8), yrow)],
            ss.at[j], rs.at[j], device_id={"pz": to}, device_id_type=MESH)

    def await_all(src, dst, ss, rs, j, axis, me, size, rows):
        at = pl.ds(pl.multiple_of(j * crow, 8), rows)
        pltpu.make_async_remote_copy(src.at[at], dst.at[at], ss.at[j], rs.at[j],
                                     device_id={axis: lax.rem(me + 1, size)}, device_id_type=MESH).wait()

    def own(src, dst, j, mine, rows):
        at = pl.ds(pl.multiple_of(j * crow + mine * rows, 8), rows)
        dst[at, :] = src[at, :]

    xf = functools.partial(x_copy, abuf, bbuf, xs, xr)
    yf = functools.partial(y_copy, abuf, cbuf, ys, yr)
    yi = functools.partial(y_copy, cbuf, dbuf, yis, yir)
    xi = functools.partial(x_copy, bbuf, ebuf, xis, xir)
    xf_wait = lambda j: await_all(abuf, bbuf, xs, xr, j, "py", py, ny, (ny - 1) * xrow)
    yf_wait = lambda j: await_all(abuf, cbuf, ys, yr, j, "pz", pz, nz, (nz - 1) * yrow)
    yi_wait = lambda j: await_all(cbuf, dbuf, yis, yir, j, "pz", pz, nz, (nz - 1) * yrow)
    xi_wait = lambda j: await_all(bbuf, ebuf, xis, xir, j, "py", py, ny, (ny - 1) * xrow)

    def x_prefetch(first):
        for k in range(SLOTS - 1):
            for c in range(2):
                rho_copy(c, first + k).start()

    def x_forward(p, first, stop):
        def body(pair, carry):
            @pl.when(pair + SLOTS - 1 < stop)
            def _():
                for c in range(2):
                    rho_copy(c, pair + SLOTS - 1).start()

            for c in range(2):
                rho_copy(c, pair).wait()
            slot = lax.rem(pair, SLOTS)
            folded = []
            for c in range(2):
                lines = stage[slot, c]
                low, high = lines[..., :half], lines[..., half:]
                both = low - high if p else low + high
                folded.append(jnp.swapaxes(both, 0, 1).reshape(2 * nf * zl, half))
            out = dot(wx[p], jnp.concatenate(folded, axis=1), ((1,), (1,)))
            blocks = swap_rows(out[:, :LANES], out[:, LANES:])
            for jj in range(HALF_X_CHUNKS):
                for to in range(ny):
                    r = jj * ny + to
                    at = (p * HALF_X_CHUNKS + jj) * crow + to * xrow + pair * 8
                    abuf[pl.ds(pl.multiple_of(at, 8), 8), :] = blocks[r % 2][r // 2]
            if p == 0:
                @pl.when(lax.rem(pair, quarter) == quarter - 1)
                def _():
                    for o in x_offsets:
                        xf(0, o, (pair - (quarter - 1)) * 8, quarter * 8).start()
            return carry

        lax.fori_loop(first, stop, body, 0)

    def y_forward(j):
        own(abuf, bbuf, j, py, xrow)
        base = j * crow
        parts = []
        for c in range(2):
            parts.append(jnp.concatenate(
                [bbuf[pl.ds(base + c * kc + i, n, stride=2 * kc), :] for i in range(2)], axis=1))
        for p in range(2):
            folded = jnp.concatenate([v[:half] - v[half:] if p else v[:half] + v[half:] for v in parts], axis=0)
            out = dot(wy[p], folded)
            for c in range(2):
                for to in range(nz):
                    for k in range(2):
                        at = base + to * yrow + (c * kc + k) * zl + p
                        abuf[pl.ds(at, zl // 2, stride=2), :] = out[
                            c * half + to * zl // 2:c * half + (to + 1) * zl // 2, k * LANES:(k + 1) * LANES]

    def z_solve(j):
        own(abuf, cbuf, j, pz, yrow)
        base, slot = j * crow, lax.rem(j, 2)
        p, jj = j // HALF_X_CHUNKS, lax.rem(j, HALF_X_CHUNKS)
        rows = kc * zl
        left = lax.broadcasted_iota(jnp.int32, (rows, LANES), 1) < zl
        swap = lambda v: pltpu.roll(v, zl, 1)
        lines = ([], [])
        for b in range(nz):
            at = base + b * yrow
            re = cbuf[pl.ds(pl.multiple_of(at, 8), rows), :]
            im = cbuf[pl.ds(pl.multiple_of(at + rows, 8), rows), :]
            lines[0].append(jnp.where(left, re, swap(im)))
            lines[1].append(jnp.where(left, swap(re), im))
        both = jnp.concatenate([jnp.concatenate(v, axis=1) for v in lines], axis=0)
        spec = dot(both, wz[...])
        gr = gbuf[slot, 0].reshape(rows, n)
        gi = gbuf[slot, 1].reshape(rows, n)
        scaled = []
        for f in range(nf):
            sr, si = spec[f * rows:(f + 1) * rows, :n], spec[f * rows:(f + 1) * rows, n:]
            hr, hi = sr * gr - si * gi, sr * gi + si * gr
            hat_re[f, pl.ds(kc * jj, kc), p] = hr.reshape(kc, zl, n)
            hat_im[f, pl.ds(kc * jj, kc), p] = hi.reshape(kc, zl, n)
            scaled.append(jnp.concatenate([hr, hi], axis=1))
        back = dot(jnp.concatenate(scaled, axis=0), wzi[...])
        for b in range(nz):
            first, second = (back[f * rows:(f + 1) * rows, b * LANES:(b + 1) * LANES] for f in range(2))
            at = base + b * yrow
            cbuf[pl.ds(pl.multiple_of(at, 8), rows), :] = jnp.where(left, first, swap(second))
            cbuf[pl.ds(pl.multiple_of(at + rows, 8), rows), :] = jnp.where(left, swap(first), second)

    def y_inverse(j):
        own(cbuf, dbuf, j, pz, yrow)
        base = j * crow
        halves = []
        for p in range(2):
            lines = []
            for k in range(2):
                lines.append(jnp.concatenate(
                    [dbuf[pl.ds(base + src * yrow + (c * kc + k) * zl + p, zl // 2, stride=2), :]
                     for c in range(2) for src in range(nz)], axis=0))
            halves.append(dot(wyi[p], jnp.concatenate(lines, axis=1)))
        for s, out in enumerate((halves[0] + halves[1], halves[0] - halves[1])):
            for c in range(2):
                for k in range(2):
                    at = base + s * (ny // 2) * xrow + c * kc + k
                    bbuf[pl.ds(at, half, stride=2 * kc), :] = out[
                        c * half:(c + 1) * half, k * LANES:(k + 1) * LANES]

    x_prefetch(0)
    tables[0].start()
    for c in range(2):
        g_copy(c, 0).start()
        g_copy(c, 1).start()
    for table in tables[1:]:
        table.start()
    pl.semaphore_wait(barrier, ny + nz - 2)
    tables[0].wait()
    x_forward(0, 0, pairs)
    x_prefetch(0)
    for jj in range(1, HALF_X_CHUNKS):
        for o in x_offsets:
            xf(jj, o).start()
    for table in tables[1:]:
        table.wait()

    def step(t, carry):
        @pl.when(t < nj)
        def _():
            xf_wait(t)
            y_forward(t)
            for o in y_offsets:
                yf(t, o).start()

        @pl.when((t >= 1) & (t < nj + 1))
        def _():
            j = t - 1
            yf_wait(j)
            for c in range(2):
                g_copy(c, j).wait()
            z_solve(j)
            for o in y_offsets:
                yi(j, o).start()

            @pl.when(j + 2 < nj)
            def _():
                for c in range(2):
                    g_copy(c, j + 2).start()

        @pl.when(t >= 2)
        def _():
            j = t - 2
            yi_wait(j)
            y_inverse(j)
            for o in x_offsets:
                xi(j, o).start()
            own(bbuf, ebuf, j, py, xrow)

        @pl.when(t < 4)
        def _():
            x_forward(1, t * quarter, (t + 1) * quarter)

            @pl.when(t < 3)
            def _():
                x_prefetch((t + 1) * quarter)

        @pl.when(t == 3)
        def _():
            def send(jj, c):
                for o in x_offsets:
                    xf(jj, o).start()
                return c

            lax.fori_loop(HALF_X_CHUNKS, nj, send, 0)

        @pl.when(t == nj - 4)
        def _():
            for jj in range(HALF_X_CHUNKS):
                xi_wait(jj)

        @pl.when((t >= nj - 4) & (t < nj))
        def _():
            def body(k, c):
                pair = (t - (nj - 4)) * quarter + k
                even[pair] = x_inverse(ebuf, wxi, 0, pair, ny, crow, xrow)
                return c

            lax.fori_loop(0, quarter, body, 0)

        return carry

    lax.fori_loop(0, nj + 2, step, 0)
    for jj in range(HALF_X_CHUNKS, nj):
        xi_wait(jj)


def x_inverse(ebuf, wxi, p, pair, ny, crow, xrow):
    tiles = [ebuf[pl.ds(pl.multiple_of((p * HALF_X_CHUNKS + jj) * crow + src * xrow + pair * 8, 8), 8), :]
             for jj in range(HALF_X_CHUNKS) for src in range(ny)]
    first, second = swap_rows(jnp.concatenate(tiles[::2], axis=0), jnp.concatenate(tiles[1::2], axis=0))
    lines = [first.reshape(-1, LANES), second.reshape(-1, LANES)]
    return dot(jnp.concatenate(lines, axis=1), wxi[p], ((0,), (0,)))


def finish(ny, n, nf, ebuf, even, hat_re, hat_im, wxi, phi_re, phi_im, out_re, out_im, stage, p_sem, h_sem):
    half = n // 2
    yl = n // ny
    nj, pairs = 2 * HALF_X_CHUNKS, yl // 2
    crow = ebuf.shape[0] // nj
    xrow = crow // ny
    zl = phi_re.shape[2]
    phi = (phi_re, phi_im)
    hats = [pltpu.make_async_copy(a, b, h_sem.at[c]) for c, (a, b) in enumerate(((hat_re, out_re), (hat_im, out_im)))]
    for h in hats:
        h.start()

    def phi_copy(c, pair):
        slot = lax.rem(pair, 2)
        return pltpu.make_async_copy(stage.at[slot, c], phi[c].at[:, pl.ds(2 * pair, 2)], p_sem.at[slot, c])

    def body(pair, carry):
        slot = lax.rem(pair, 2)
        e, o = even[pair], x_inverse(ebuf, wxi, 1, pair, ny, crow, xrow)

        @pl.when(pair >= 2)
        def _():
            for c in range(2):
                phi_copy(c, pair - 2).wait()

        for c in range(2):
            ec, oc = e[:, c * half:(c + 1) * half], o[:, c * half:(c + 1) * half]
            out = jnp.concatenate([ec + oc, ec - oc], axis=1).reshape(2, nf, zl, n)
            stage[slot, c] = jnp.swapaxes(out, 0, 1)
            phi_copy(c, pair).start()
        return carry

    lax.fori_loop(0, pairs, body, 0)
    for pair in (pairs - 2, pairs - 1):
        for c in range(2):
            phi_copy(c, pair).wait()
    for h in hats:
        h.wait()


def solution(mesh):
    ny, nz = mesh.shape["py"], mesh.shape["pz"]

    def local_solve(rho_re, rho_im, g_re, g_im):
        nf, n, yl, zl = rho_re.shape
        kl, ml = g_re.shape[:2]
        kc = kl // HALF_X_CHUNKS // 2
        nj = 2 * HALF_X_CHUNKS
        rows = nj * ny * yl * 2 * kc
        tables = [jnp.asarray(w) for w in dft_tables(n, ny, nz)]
        space = jax.ShapeDtypeStruct((nf, yl, zl, n), jnp.float32)
        wave_shape = (nf, kl // 2, 2, ml, n)
        wave = jax.ShapeDtypeStruct(wave_shape, jnp.float32)
        dma = pltpu.SemaphoreType.DMA
        buf = pltpu.VMEM((rows, LANES), jnp.float32)
        vmem = pl.BlockSpec(memory_space=pltpu.VMEM)
        hbm = pl.BlockSpec(memory_space=pl.ANY)
        inner = pl.pallas_call(
            functools.partial(kernel, ny, nz, n, nf),
            out_shape=(pltpu.VMEM((rows, LANES), jnp.float32), pltpu.VMEM((yl // 2, 2 * nf * zl, n), jnp.float32),
                       pltpu.VMEM(wave_shape, jnp.float32), pltpu.VMEM(wave_shape, jnp.float32)),
            in_specs=[hbm] * 10,
            out_specs=[vmem] * 4,
            scratch_shapes=[
                buf, buf, buf, buf,
                pltpu.VMEM((SLOTS, 2, nf, 2, zl, n), jnp.float32),
                pltpu.VMEM((2, 2, kc, ml, n), jnp.float32),
                *[pltpu.VMEM(t.shape, jnp.float32) for t in tables],
                *[dma((nj,)) for _ in range(8)],
                dma((len(tables),)), dma((SLOTS, 2)), dma((2, 2)),
            ],
            compiler_params=pltpu.CompilerParams(
                collective_id=0, has_side_effects=True, vmem_limit_bytes=INNER_VMEM),
            name="spectral",
        )(jnp.transpose(rho_re, (0, 2, 3, 1)), jnp.transpose(rho_im, (0, 2, 3, 1)),
          g_re.reshape(kl // 2, 2, ml, n), g_im.reshape(kl // 2, 2, ml, n), *tables)
        outs = pl.pallas_call(
            functools.partial(finish, ny, n, nf),
            out_shape=(space, space, wave, wave),
            in_specs=[vmem] * 5,
            out_specs=[hbm] * 4,
            scratch_shapes=[pltpu.VMEM((2, 2, nf, 2, zl, n), jnp.float32), dma((2, 2)), dma((2,))],
            compiler_params=pltpu.CompilerParams(vmem_limit_bytes=16 << 20),
            name="finish",
        )(*inner, tables[5])
        phi = [jnp.transpose(v, (0, 3, 1, 2)) for v in outs[:2]]
        return (*phi, *(v.reshape(nf, kl, ml, n) for v in outs[2:]))

    space_layout = P("dp", None, "py", "pz")
    wave_layout = P("dp", "py", "pz", None)
    green_layout = P("py", "pz", None)
    return jax.shard_map(local_solve, mesh=mesh,
                         in_specs=(space_layout, space_layout, green_layout, green_layout),
                         out_specs=(space_layout, space_layout, wave_layout, wave_layout),
                         check_vma=False)
```

time: 268 us -> 223 us (0.83)
  Pallas kernels: 253 us -> 222 us
  local copies, waits for them, and re-layouts: 14.3 us -> 0.01 us
    pallas_call x1 -> x2, Pallas kernels: 253 us -> 222 us  [the longest x1 212 us: local_solve(): pl.pallas_call(functools.partial(kernel, ny, nz, n, nf), out_shape=(pltpu...]
    unnamed x10 -> x2, local copies, waits for them, and re-layouts: 14.3 us -> 0.01 us
where the time goes in v2:
time: 223 us
  Pallas kernels  222 us (100%)
    pallas_call x1, Pallas kernels, local_solve(): pl.pallas_call(functools.partial(kernel, ny, nz, n, nf), out_shape=(pltpu...  212 us
    pallas_call x1, Pallas kernels, local_solve(): pl.pallas_call(functools.partial(finish, ny, n, nf), out_shape=(space, sp...  10.6 us

profile of v2, /device:TPU:97, one launch (start us, length us, event | category | flops | bytes accessed | tf_op | source)
XLA Modules:
  0.0 222.8 jit_solution(7255464715760739976)
XLA Ops:
  0.6 0.0 copy-start
  0.6 211.5 %spectral.1 = (f32[16384,128]{1,0:T(8,128)S(1)}, f32[16,256,256]{2,1,0:T(8,128)S(1)}, f32[2,16,2,64,256]{4,3,2,1,0:T(8,128)S(1)}, f32[2,16,2,64,256]{4,3,2,1,0:T(8,128)S(1)}) custom-call(f32[2,32,64,256]{3,2,1,0:T(8,128)} %bitcast.8, f32[2,32,64,256]{3,2,1,0:T(8,128)} %bitcast.9, f32[16,2,64,256]{3,2,1,0:T(8,128)} %bitcast.10, f32[16,2,64,256]{3,2,1,0:T(8,128)} %bitcast.11, ...), custom_call_target="tpu_custom_call" | custom-call | tf_op jit(solution)/shard_map/spectral/pallas_call | solution.py:377
  212.2 0.0 copy-done
  212.2 10.6 %finish.1 = (f32[2,32,64,256]{3,2,1,0:T(8,128)}, f32[2,32,64,256]{3,2,1,0:T(8,128)}, f32[2,16,2,64,256]{4,3,2,1,0:T(8,128)}, f32[2,16,2,64,256]{4,3,2,1,0:T(8,128)}) custom-call(f32[16384,128]{1,0:T(8,128)S(1)} %get-tuple-element.12.ebuf, f32[16,256,256]{2,1,0:T(8,128)S(1)} %get-tuple-element.13.even, f32[2,16,2,64,256]{4,3,2,1,0:T(8,128)S(1)} %get-tuple-element.14.hat_re, ...), custom_call_target="tpu_custom_call" | custom-call | tf_op jit(solution)/shard_map/finish/pallas_call | solution.py:396
Async XLA Ops:
  0.6 211.6 %copy-start = (f32[2,256,256]{2,1,0:T(8,128)S(1)}, f32[2,256,256]{2,1,0:T(8,128)}, u32[]{:S(2)}) copy-start(f32[2,256,256]{2,1,0:T(8,128)} %constant.17.clone.wxi_h.wxi) | copy-start | bytes 1572868

commit v3 on v2

--- a/solution.py
+++ b/solution.py
@@ -10,7 +10,9 @@
 
 MESH = pl.DeviceIdType.MESH
 HALF_X_CHUNKS = 8
-SLOTS = 4
+SLOTS = 3
+GROUP = 2
+OUT_SLOTS = 8
 LANES = 128
 INNER_VMEM = 42 << 20
 
@@ -28,15 +30,13 @@
     order = np.arange(half).reshape(ny, HALF_X_CHUNKS, per).transpose(1, 0, 2)
     rows = np.stack([order, order + half], axis=2).reshape(-1)
     wx = np.stack([real_form(dft(2 * low + p, low, -1))[rows] for p in range(2)])
-    wxi = np.stack([real_form(dft(low, 2 * low + p, 1))[:, rows].T for p in range(2)])
     wy = np.stack([real_form(dft(2 * low + p, low, -1)) for p in range(2)])
     wyi = np.stack([real_form(dft(low, 2 * low + p, 1)) for p in range(2)])
     lz = n // nz
     zrows = np.arange(n).reshape(nz, lz)
     zrows = np.stack([zrows, zrows + n], axis=1).reshape(-1)
     wz = real_form(dft(full, full, -1)).T[zrows]
-    wzi = real_form(dft(full, full, 1)).T[:, zrows]
-    return [np.asarray(w, np.float32) for w in (wx, wy, wz, wzi, wyi, wxi)]
+    return [np.asarray(w, np.float32) for w in (wx, wy, wz, wyi)]
 
 
 def dot(a, b, dims=((1,), (0,))):
@@ -51,9 +51,9 @@
 
 
 def kernel(ny, nz, n, nf,
-           rho_re, rho_im, g_re, g_im, wx_h, wy_h, wz_h, wzi_h, wyi_h, wxi_h,
+           rho_re, rho_im, g_re, g_im, wx_h, wy_h, wz_h, wyi_h,
            ebuf, even, hat_re, hat_im,
-           abuf, bbuf, cbuf, dbuf, stage, gbuf, wx, wy, wz, wzi, wyi, wxi,
+           abuf, bbuf, cbuf, dbuf, stage, gbuf, wx, wy, wz, wyi,
            xs, xr, ys, yr, yis, yir, xis, xir, w_sem, in_sem, g_sem):
     py, pz = lax.axis_index("py"), lax.axis_index("pz")
     half = n // 2
@@ -64,22 +64,20 @@
     crow = ny * xrow
     pairs = yl // 2
     quarter = pairs // 4
+    groups = pairs // GROUP
+    piece = groups // 4
     rho, gg, hat = (rho_re, rho_im), (g_re, g_im), (hat_re, hat_im)
     x_offsets = (4, 3, 5, 2, 6, 1, 7) if ny == 8 else tuple(range(1, ny))
     y_offsets = (2, 1, 3) if nz == 4 else tuple(range(1, nz))
 
     barrier = pltpu.get_barrier_semaphore()
-    for o in range(1, ny):
-        pl.semaphore_signal(barrier, inc=1, device_id={"py": lax.rem(py + o, ny)}, device_id_type=MESH)
-    for o in range(1, nz):
-        pl.semaphore_signal(barrier, inc=1, device_id={"pz": lax.rem(pz + o, nz)}, device_id_type=MESH)
-
     tables = [pltpu.make_async_copy(h, v, w_sem.at[i]) for i, (h, v) in enumerate(
-        ((wx_h, wx), (wy_h, wy), (wz_h, wz), (wzi_h, wzi), (wyi_h, wyi), (wxi_h, wxi)))]
-
-    def rho_copy(c, pair):
-        slot = lax.rem(pair, SLOTS)
-        return pltpu.make_async_copy(rho[c].at[:, pl.ds(2 * pair, 2)], stage.at[slot, c], in_sem.at[slot, c])
+        ((wx_h, wx), (wy_h, wy), (wz_h, wz), (wyi_h, wyi)))]
+
+    def rho_copy(c, group):
+        slot = lax.rem(group, SLOTS)
+        return pltpu.make_async_copy(rho[c].at[:, pl.ds(2 * GROUP * group, 2 * GROUP)], stage.at[slot, c],
+                                     in_sem.at[slot, c])
 
     def g_copy(c, j):
         p, jj, slot = j // HALF_X_CHUNKS, lax.rem(j, HALF_X_CHUNKS), lax.rem(j, 2)
@@ -124,33 +122,36 @@
                 rho_copy(c, first + k).start()
 
     def x_forward(p, first, stop):
-        def body(pair, carry):
-            @pl.when(pair + SLOTS - 1 < stop)
+        def body(group, carry):
+            @pl.when(group + SLOTS - 1 < stop)
             def _():
                 for c in range(2):
-                    rho_copy(c, pair + SLOTS - 1).start()
-
-            for c in range(2):
-                rho_copy(c, pair).wait()
-            slot = lax.rem(pair, SLOTS)
-            folded = []
-            for c in range(2):
-                lines = stage[slot, c]
-                low, high = lines[..., :half], lines[..., half:]
-                both = low - high if p else low + high
-                folded.append(jnp.swapaxes(both, 0, 1).reshape(2 * nf * zl, half))
-            out = dot(wx[p], jnp.concatenate(folded, axis=1), ((1,), (1,)))
-            blocks = swap_rows(out[:, :LANES], out[:, LANES:])
-            for jj in range(HALF_X_CHUNKS):
-                for to in range(ny):
-                    r = jj * ny + to
-                    at = (p * HALF_X_CHUNKS + jj) * crow + to * xrow + pair * 8
-                    abuf[pl.ds(pl.multiple_of(at, 8), 8), :] = blocks[r % 2][r // 2]
+                    rho_copy(c, group + SLOTS - 1).start()
+
+            for c in range(2):
+                rho_copy(c, group).wait()
+            slot = lax.rem(group, SLOTS)
+            for u in range(GROUP):
+                folded = []
+                for c in range(2):
+                    lines = stage[slot, c, :, 2 * u:2 * u + 2]
+                    low, high = lines[..., :half], lines[..., half:]
+                    both = low - high if p else low + high
+                    folded.append(jnp.swapaxes(both, 0, 1).reshape(2 * nf * zl, half))
+                out = dot(wx[p], jnp.concatenate(folded, axis=1), ((1,), (1,)))
+                blocks = swap_rows(out[:, :LANES], out[:, LANES:])
+                for jj in range(HALF_X_CHUNKS):
+                    for to in range(ny):
+                        r = jj * ny + to
+                        at = (p * HALF_X_CHUNKS + jj) * crow + to * xrow + (group * GROUP + u) * 8
+                        abuf[pl.ds(pl.multiple_of(at, 8), 8), :] = blocks[r % 2][r // 2]
             if p == 0:
-                @pl.when(lax.rem(pair, quarter) == quarter - 1)
+                @pl.when(group == first)
                 def _():
-                    for o in x_offsets:
-                        xf(0, o, (pair - (quarter - 1)) * 8, quarter * 8).start()
+                    pl.semaphore_wait(barrier, ny + nz - 2)
+
+                for o in x_offsets:
+                    xf(0, o, group * GROUP * 8, GROUP * 8).start()
             return carry
 
         lax.fori_loop(first, stop, body, 0)
@@ -197,7 +198,7 @@
             hat_re[f, pl.ds(kc * jj, kc), p] = hr.reshape(kc, zl, n)
             hat_im[f, pl.ds(kc * jj, kc), p] = hi.reshape(kc, zl, n)
             scaled.append(jnp.concatenate([hr, hi], axis=1))
-        back = dot(jnp.concatenate(scaled, axis=0), wzi[...])
+        back = dot(jnp.concatenate(scaled, axis=0), wz[...], ((1,), (1,)))
         for b in range(nz):
             first, second = (back[f * rows:(f + 1) * rows, b * LANES:(b + 1) * LANES] for f in range(2))
             at = base + b * yrow
@@ -224,14 +225,17 @@
 
     x_prefetch(0)
     tables[0].start()
+    for o in range(1, ny):
+        pl.semaphore_signal(barrier, inc=1, device_id={"py": lax.rem(py + o, ny)}, device_id_type=MESH)
+    for o in range(1, nz):
+        pl.semaphore_signal(barrier, inc=1, device_id={"pz": lax.rem(pz + o, nz)}, device_id_type=MESH)
+    tables[0].wait()
+    x_forward(0, 0, groups)
     for c in range(2):
         g_copy(c, 0).start()
         g_copy(c, 1).start()
     for table in tables[1:]:
         table.start()
-    pl.semaphore_wait(barrier, ny + nz - 2)
-    tables[0].wait()
-    x_forward(0, 0, pairs)
     x_prefetch(0)
     for jj in range(1, HALF_X_CHUNKS):
         for o in x_offsets:
@@ -273,11 +277,11 @@
 
         @pl.when(t < 4)
         def _():
-            x_forward(1, t * quarter, (t + 1) * quarter)
+            x_forward(1, t * piece, (t + 1) * piece)
 
             @pl.when(t < 3)
             def _():
-                x_prefetch((t + 1) * quarter)
+                x_prefetch((t + 1) * piece)
 
         @pl.when(t == 3)
         def _():
@@ -297,7 +301,7 @@
         def _():
             def body(k, c):
                 pair = (t - (nj - 4)) * quarter + k
-                even[pair] = x_inverse(ebuf, wxi, 0, pair, ny, crow, xrow)
+                even[pair] = x_inverse(ebuf, wx, 0, pair, ny, crow, xrow)
                 return c
 
             lax.fori_loop(0, quarter, body, 0)
@@ -309,15 +313,15 @@
         xi_wait(jj)
 
 
-def x_inverse(ebuf, wxi, p, pair, ny, crow, xrow):
+def x_inverse(ebuf, wx, p, pair, ny, crow, xrow):
     tiles = [ebuf[pl.ds(pl.multiple_of((p * HALF_X_CHUNKS + jj) * crow + src * xrow + pair * 8, 8), 8), :]
              for jj in range(HALF_X_CHUNKS) for src in range(ny)]
     first, second = swap_rows(jnp.concatenate(tiles[::2], axis=0), jnp.concatenate(tiles[1::2], axis=0))
     lines = [first.reshape(-1, LANES), second.reshape(-1, LANES)]
-    return dot(jnp.concatenate(lines, axis=1), wxi[p], ((0,), (0,)))
-
-
-def finish(ny, n, nf, ebuf, even, hat_re, hat_im, wxi, phi_re, phi_im, out_re, out_im, stage, p_sem, h_sem):
+    return dot(jnp.concatenate(lines, axis=1), wx[p], ((0,), (0,)))
+
+
+def finish(ny, n, nf, ebuf, even, hat_re, hat_im, wx, phi_re, phi_im, out_re, out_im, stage, p_sem, h_sem):
     half = n // 2
     yl = n // ny
     nj, pairs = 2 * HALF_X_CHUNKS, yl // 2
@@ -330,27 +334,31 @@
         h.start()
 
     def phi_copy(c, pair):
-        slot = lax.rem(pair, 2)
+        slot = lax.rem(pair, OUT_SLOTS)
         return pltpu.make_async_copy(stage.at[slot, c], phi[c].at[:, pl.ds(2 * pair, 2)], p_sem.at[slot, c])
 
-    def body(pair, carry):
-        slot = lax.rem(pair, 2)
-        e, o = even[pair], x_inverse(ebuf, wxi, 1, pair, ny, crow, xrow)
-
-        @pl.when(pair >= 2)
-        def _():
-            for c in range(2):
-                phi_copy(c, pair - 2).wait()
-
-        for c in range(2):
-            ec, oc = e[:, c * half:(c + 1) * half], o[:, c * half:(c + 1) * half]
-            out = jnp.concatenate([ec + oc, ec - oc], axis=1).reshape(2, nf, zl, n)
-            stage[slot, c] = jnp.swapaxes(out, 0, 1)
-            phi_copy(c, pair).start()
+    def body(group, carry):
+        @pl.when(group * GROUP >= OUT_SLOTS)
+        def _():
+            for u in range(GROUP):
+                for c in range(2):
+                    phi_copy(c, group * GROUP + u - OUT_SLOTS).wait()
+
+        for u in range(GROUP):
+            pair = group * GROUP + u
+            slot = lax.rem(pair, OUT_SLOTS)
+            e, o = even[pair], x_inverse(ebuf, wx, 1, pair, ny, crow, xrow)
+            for c in range(2):
+                ec, oc = e[:, c * half:(c + 1) * half], o[:, c * half:(c + 1) * half]
+                out = jnp.concatenate([ec + oc, ec - oc], axis=1).reshape(2, nf, zl, n)
+                stage[slot, c] = jnp.swapaxes(out, 0, 1)
+        for u in range(GROUP):
+            for c in range(2):
+                phi_copy(c, group * GROUP + u).start()
         return carry
 
-    lax.fori_loop(0, pairs, body, 0)
-    for pair in (pairs - 2, pairs - 1):
+    lax.fori_loop(0, pairs // GROUP, body, 0)
+    for pair in range(pairs - OUT_SLOTS, pairs):
         for c in range(2):
             phi_copy(c, pair).wait()
     for h in hats:
@@ -378,11 +386,11 @@
             functools.partial(kernel, ny, nz, n, nf),
             out_shape=(pltpu.VMEM((rows, LANES), jnp.float32), pltpu.VMEM((yl // 2, 2 * nf * zl, n), jnp.float32),
                        pltpu.VMEM(wave_shape, jnp.float32), pltpu.VMEM(wave_shape, jnp.float32)),
-            in_specs=[hbm] * 10,
+            in_specs=[hbm] * 8,
             out_specs=[vmem] * 4,
             scratch_shapes=[
                 buf, buf, buf, buf,
-                pltpu.VMEM((SLOTS, 2, nf, 2, zl, n), jnp.float32),
+                pltpu.VMEM((SLOTS, 2, nf, 2 * GROUP, zl, n), jnp.float32),
                 pltpu.VMEM((2, 2, kc, ml, n), jnp.float32),
                 *[pltpu.VMEM(t.shape, jnp.float32) for t in tables],
                 *[dma((nj,)) for _ in range(8)],
@@ -398,10 +406,10 @@
             out_shape=(space, space, wave, wave),
             in_specs=[vmem] * 5,
             out_specs=[hbm] * 4,
-            scratch_shapes=[pltpu.VMEM((2, 2, nf, 2, zl, n), jnp.float32), dma((2, 2)), dma((2,))],
+            scratch_shapes=[pltpu.VMEM((OUT_SLOTS, 2, nf, 2, zl, n), jnp.float32), dma((OUT_SLOTS, 2)), dma((2,))],
             compiler_params=pltpu.CompilerParams(vmem_limit_bytes=16 << 20),
             name="finish",
-        )(*inner, tables[5])
+        )(*inner, tables[0])
         phi = [jnp.transpose(v, (0, 3, 1, 2)) for v in outs[:2]]
         return (*phi, *(v.reshape(nf, kl, ml, n) for v in outs[2:]))
 

time: 223 us -> 218 us (0.978)
  Pallas kernels: 222 us -> 217 us
    pallas_call x1, Pallas kernels: 10.6 us -> 7.55 us  [local_solve(): pl.pallas_call(functools.partial(finish, ny, n, nf), out_shape=(space, sp...]
    pallas_call x1, Pallas kernels: 212 us -> 209 us  [local_solve(): pl.pallas_call(functools.partial(kernel, ny, nz, n, nf), out_shape=(pltpu...]
where the time goes in v3:
time: 218 us; the launch traced here: 217 us
  Pallas kernels  217 us (100%)
    pallas_call x1, Pallas kernels, local_solve(): pl.pallas_call(functools.partial(kernel, ny, nz, n, nf), out_shape=(pltpu...  209 us
    pallas_call x1, Pallas kernels, local_solve(): pl.pallas_call(functools.partial(finish, ny, n, nf), out_shape=(space, sp...  7.55 us

profile of v3, /device:TPU:97, one launch (start us, length us, event | category | flops | bytes accessed | tf_op | source)
XLA Modules:
  0.0 217.3 jit_solution(11390320676386955758)
XLA Ops:
  0.6 0.0 copy-start
  0.6 209.0 %spectral.1 = (f32[16384,128]{1,0:T(8,128)S(1)}, f32[16,256,256]{2,1,0:T(8,128)S(1)}, f32[2,16,2,64,256]{4,3,2,1,0:T(8,128)S(1)}, f32[2,16,2,64,256]{4,3,2,1,0:T(8,128)S(1)}) custom-call(f32[2,32,64,256]{3,2,1,0:T(8,128)} %bitcast.8, f32[2,32,64,256]{3,2,1,0:T(8,128)} %bitcast.9, f32[16,2,64,256]{3,2,1,0:T(8,128)} %bitcast.10, f32[16,2,64,256]{3,2,1,0:T(8,128)} %bitcast.11, ...), custom_call_target="tpu_custom_call" | custom-call | tf_op jit(solution)/shard_map/spectral/pallas_call | solution.py:385
  209.7 0.0 copy-done
  209.7 7.5 %finish.1 = (f32[2,32,64,256]{3,2,1,0:T(8,128)}, f32[2,32,64,256]{3,2,1,0:T(8,128)}, f32[2,16,2,64,256]{4,3,2,1,0:T(8,128)}, f32[2,16,2,64,256]{4,3,2,1,0:T(8,128)}) custom-call(f32[16384,128]{1,0:T(8,128)S(1)} %get-tuple-element.12.ebuf, f32[16,256,256]{2,1,0:T(8,128)S(1)} %get-tuple-element.13.even, f32[2,16,2,64,256]{4,3,2,1,0:T(8,128)S(1)} %get-tuple-element.14.hat_re, ...), custom_call_target="tpu_custom_call" | custom-call | tf_op jit(solution)/shard_map/finish/pallas_call | solution.py:404
Async XLA Ops:
  0.6 209.1 %copy-start = (f32[2,256,256]{2,1,0:T(8,128)S(1)}, f32[2,256,256]{2,1,0:T(8,128)}, u32[]{:S(2)}) copy-start(f32[2,256,256]{2,1,0:T(8,128)} %constant.8.clone.wx_h.wx) | copy-start | bytes 1572868

commit v4 on v3

--- a/solution.py
+++ b/solution.py
@@ -12,7 +12,7 @@
 HALF_X_CHUNKS = 8
 SLOTS = 3
 GROUP = 2
-OUT_SLOTS = 8
+OUT_SLOTS = 4
 LANES = 128
 INNER_VMEM = 42 << 20
 
@@ -28,7 +28,7 @@
     dft = lambda k, j, sign: scale * np.exp(sign * 2j * np.pi * ((k[:, None] * j[None, :]) % n) / n)
     per = n // ny // HALF_X_CHUNKS // 2
     order = np.arange(half).reshape(ny, HALF_X_CHUNKS, per).transpose(1, 0, 2)
-    rows = np.stack([order, order + half], axis=2).reshape(-1)
+    rows = np.stack([order, order + half], axis=3).reshape(-1)
     wx = np.stack([real_form(dft(2 * low + p, low, -1))[rows] for p in range(2)])
     wy = np.stack([real_form(dft(2 * low + p, low, -1)) for p in range(2)])
     wyi = np.stack([real_form(dft(low, 2 * low + p, 1)) for p in range(2)])
@@ -48,6 +48,11 @@
     a, b = first.reshape(-1, 8, LANES), second.reshape(-1, 8, LANES)
     upper = lax.broadcasted_iota(jnp.int32, a.shape, 1) < 4
     return jnp.where(upper, a, pltpu.roll(b, 4, 1)), jnp.where(upper, pltpu.roll(a, 4, 1), b)
+
+
+def swap_pairs(a, b):
+    kept = lax.broadcasted_iota(jnp.int32, a.shape, 1) & 2 == 0
+    return jnp.where(kept, a, pltpu.roll(b, 2, 1)), jnp.where(kept, pltpu.roll(a, 6, 1), b)
 
 
 def kernel(ny, nz, n, nf,
@@ -63,9 +68,9 @@
     xrow, yrow = yl * 2 * kc, 2 * kc * zl
     crow = ny * xrow
     pairs = yl // 2
-    quarter = pairs // 4
     groups = pairs // GROUP
     piece = groups // 4
+    sends = ((0, groups // 2), (groups // 2, piece), (groups - piece, piece // 2), (groups - piece // 2, piece // 2))
     rho, gg, hat = (rho_re, rho_im), (g_re, g_im), (hat_re, hat_im)
     x_offsets = (4, 3, 5, 2, 6, 1, 7) if ny == 8 else tuple(range(1, ny))
     y_offsets = (2, 1, 3) if nz == 4 else tuple(range(1, nz))
@@ -83,24 +88,25 @@
         p, jj, slot = j // HALF_X_CHUNKS, lax.rem(j, HALF_X_CHUNKS), lax.rem(j, 2)
         return pltpu.make_async_copy(gg[c].at[pl.ds(kc * jj, kc), p], gbuf.at[slot, c], g_sem.at[slot, c])
 
-    def x_copy(src, dst, ss, rs, j, o, first=0, count=None):
+    def x_copy(src, dst, ss, rs, j, o, first=0, count=None, *half_of):
         to = lax.rem(py + o, ny)
         rows = xrow if count is None else count
         return pltpu.make_async_remote_copy(
             src.at[pl.ds(pl.multiple_of(j * crow + to * xrow + first, 8), rows)],
             dst.at[pl.ds(pl.multiple_of(j * crow + py * xrow + first, 8), rows)],
-            ss.at[j], rs.at[j], device_id={"py": to}, device_id_type=MESH)
-
-    def y_copy(src, dst, ss, rs, j, o):
+            ss.at[j, *half_of], rs.at[j, *half_of], device_id={"py": to}, device_id_type=MESH)
+
+    def y_copy(src, dst, ss, rs, j, o, first=0, count=None, *half_of):
         to = lax.rem(pz + o, nz)
+        rows = yrow if count is None else count
         return pltpu.make_async_remote_copy(
-            src.at[pl.ds(pl.multiple_of(j * crow + to * yrow, 8), yrow)],
-            dst.at[pl.ds(pl.multiple_of(j * crow + pz * yrow, 8), yrow)],
-            ss.at[j], rs.at[j], device_id={"pz": to}, device_id_type=MESH)
-
-    def await_all(src, dst, ss, rs, j, axis, me, size, rows):
-        at = pl.ds(pl.multiple_of(j * crow, 8), rows)
-        pltpu.make_async_remote_copy(src.at[at], dst.at[at], ss.at[j], rs.at[j],
+            src.at[pl.ds(pl.multiple_of(j * crow + to * yrow + first, 8), rows)],
+            dst.at[pl.ds(pl.multiple_of(j * crow + pz * yrow + first, 8), rows)],
+            ss.at[j, *half_of], rs.at[j, *half_of], device_id={"pz": to}, device_id_type=MESH)
+
+    def await_all(src, dst, ss, rs, axis, me, size, rows, *of):
+        at = pl.ds(pl.multiple_of(of[0] * crow, 8), rows)
+        pltpu.make_async_remote_copy(src.at[at], dst.at[at], ss.at[*of], rs.at[*of],
                                      device_id={axis: lax.rem(me + 1, size)}, device_id_type=MESH).wait()
 
     def own(src, dst, j, mine, rows):
@@ -111,10 +117,10 @@
     yf = functools.partial(y_copy, abuf, cbuf, ys, yr)
     yi = functools.partial(y_copy, cbuf, dbuf, yis, yir)
     xi = functools.partial(x_copy, bbuf, ebuf, xis, xir)
-    xf_wait = lambda j: await_all(abuf, bbuf, xs, xr, j, "py", py, ny, (ny - 1) * xrow)
-    yf_wait = lambda j: await_all(abuf, cbuf, ys, yr, j, "pz", pz, nz, (nz - 1) * yrow)
-    yi_wait = lambda j: await_all(cbuf, dbuf, yis, yir, j, "pz", pz, nz, (nz - 1) * yrow)
-    xi_wait = lambda j: await_all(bbuf, ebuf, xis, xir, j, "py", py, ny, (ny - 1) * xrow)
+    xf_wait = functools.partial(await_all, abuf, bbuf, xs, xr, "py", py, ny, (ny - 1) * xrow)
+    yf_wait = functools.partial(await_all, abuf, cbuf, ys, yr, "pz", pz, nz, (nz - 1) * yrow)
+    yi_wait = functools.partial(await_all, cbuf, dbuf, yis, yir, "pz", pz, nz, (nz - 1) * yrow // 2)
+    xi_wait = functools.partial(await_all, bbuf, ebuf, xis, xir, "py", py, ny, (ny - 1) * xrow // 2)
 
     def x_prefetch(first):
         for k in range(SLOTS - 1):
@@ -131,27 +137,29 @@
             for c in range(2):
                 rho_copy(c, group).wait()
             slot = lax.rem(group, SLOTS)
+            folded = []
+            for c in range(2):
+                lines = stage[slot, c]
+                low, high = lines[..., :half], lines[..., half:]
+                both = low - high if p else low + high
+                folded.append(jnp.swapaxes(both, 0, 1).reshape(2 * GROUP * nf * zl, half))
+            out = dot(wx[p], jnp.concatenate(folded, axis=1), ((1,), (1,)))
             for u in range(GROUP):
-                folded = []
-                for c in range(2):
-                    lines = stage[slot, c, :, 2 * u:2 * u + 2]
-                    low, high = lines[..., :half], lines[..., half:]
-                    both = low - high if p else low + high
-                    folded.append(jnp.swapaxes(both, 0, 1).reshape(2 * nf * zl, half))
-                out = dot(wx[p], jnp.concatenate(folded, axis=1), ((1,), (1,)))
-                blocks = swap_rows(out[:, :LANES], out[:, LANES:])
+                blocks = swap_rows(out[:, 2 * u * LANES:(2 * u + 1) * LANES],
+                                   out[:, (2 * u + 1) * LANES:(2 * u + 2) * LANES])
                 for jj in range(HALF_X_CHUNKS):
                     for to in range(ny):
                         r = jj * ny + to
                         at = (p * HALF_X_CHUNKS + jj) * crow + to * xrow + (group * GROUP + u) * 8
                         abuf[pl.ds(pl.multiple_of(at, 8), 8), :] = blocks[r % 2][r // 2]
             if p == 0:
-                @pl.when(group == first)
-                def _():
-                    pl.semaphore_wait(barrier, ny + nz - 2)
-
-                for o in x_offsets:
-                    xf(0, o, group * GROUP * 8, GROUP * 8).start()
+                for start, count in sends:
+                    @pl.when(group == start + count - 1)
+                    def _():
+                        if start == 0:
+                            pl.semaphore_wait(barrier, ny + nz - 2)
+                        for o in x_offsets:
+                            xf(0, o, start * GROUP * 8, count * GROUP * 8).start()
             return carry
 
         lax.fori_loop(first, stop, body, 0)
@@ -162,7 +170,7 @@
         parts = []
         for c in range(2):
             parts.append(jnp.concatenate(
-                [bbuf[pl.ds(base + c * kc + i, n, stride=2 * kc), :] for i in range(2)], axis=1))
+                [bbuf[pl.ds(base + 2 * i + c, n, stride=2 * kc), :] for i in range(2)], axis=1))
         for p in range(2):
             folded = jnp.concatenate([v[:half] - v[half:] if p else v[:half] + v[half:] for v in parts], axis=0)
             out = dot(wy[p], folded)
@@ -205,23 +213,19 @@
             cbuf[pl.ds(pl.multiple_of(at, 8), rows), :] = jnp.where(left, first, swap(second))
             cbuf[pl.ds(pl.multiple_of(at + rows, 8), rows), :] = jnp.where(left, swap(first), second)
 
-    def y_inverse(j):
-        own(cbuf, dbuf, j, pz, yrow)
+    def y_inverse(j, i):
         base = j * crow
         halves = []
         for p in range(2):
-            lines = []
-            for k in range(2):
-                lines.append(jnp.concatenate(
-                    [dbuf[pl.ds(base + src * yrow + (c * kc + k) * zl + p, zl // 2, stride=2), :]
-                     for c in range(2) for src in range(nz)], axis=0))
-            halves.append(dot(wyi[p], jnp.concatenate(lines, axis=1)))
+            lines = jnp.concatenate(
+                [dbuf[pl.ds(base + src * yrow + (c * kc + i) * zl + p, zl // 2, stride=2), :]
+                 for c in range(2) for src in range(nz)], axis=0)
+            halves.append(dot(wyi[p], lines))
         for s, out in enumerate((halves[0] + halves[1], halves[0] - halves[1])):
             for c in range(2):
-                for k in range(2):
-                    at = base + s * (ny // 2) * xrow + c * kc + k
-                    bbuf[pl.ds(at, half, stride=2 * kc), :] = out[
-                        c * half:(c + 1) * half, k * LANES:(k + 1) * LANES]
+                for to in range(ny // 2):
+                    at = base + (s * (ny // 2) + to) * xrow + 2 * i * yl + c
+                    bbuf[pl.ds(at, yl, stride=2), :] = out[c * half + to * yl:c * half + (to + 1) * yl]
 
     x_prefetch(0)
     tables[0].start()
@@ -258,8 +262,10 @@
             for c in range(2):
                 g_copy(c, j).wait()
             z_solve(j)
-            for o in y_offsets:
-                yi(j, o).start()
+            for i in range(kc):
+                for o in y_offsets:
+                    for c in range(2):
+                        yi(j, o, (c * kc + i) * zl, zl, i).start()
 
             @pl.when(j + 2 < nj)
             def _():
@@ -269,10 +275,12 @@
         @pl.when(t >= 2)
         def _():
             j = t - 2
-            yi_wait(j)
-            y_inverse(j)
-            for o in x_offsets:
-                xi(j, o).start()
+            own(cbuf, dbuf, j, pz, yrow)
+            for i in range(kc):
+                yi_wait(j, i)
+                y_inverse(j, i)
+                for o in x_offsets:
+                    xi(j, o, 2 * i * yl, 2 * yl, i).start()
             own(bbuf, ebuf, j, py, xrow)
 
         @pl.when(t < 4)
@@ -295,36 +303,43 @@
         @pl.when(t == nj - 4)
         def _():
             for jj in range(HALF_X_CHUNKS):
-                xi_wait(jj)
+                for i in range(kc):
+                    xi_wait(jj, i)
 
         @pl.when((t >= nj - 4) & (t < nj))
         def _():
             def body(k, c):
-                pair = (t - (nj - 4)) * quarter + k
-                even[pair] = x_inverse(ebuf, wx, 0, pair, ny, crow, xrow)
+                group = (t - (nj - 4)) * piece + k
+                even[group] = x_inverse(ebuf, wx, 0, group, ny, crow, xrow)
                 return c
 
-            lax.fori_loop(0, quarter, body, 0)
+            lax.fori_loop(0, piece, body, 0)
 
         return carry
 
     lax.fori_loop(0, nj + 2, step, 0)
     for jj in range(HALF_X_CHUNKS, nj):
-        xi_wait(jj)
-
-
-def x_inverse(ebuf, wx, p, pair, ny, crow, xrow):
-    tiles = [ebuf[pl.ds(pl.multiple_of((p * HALF_X_CHUNKS + jj) * crow + src * xrow + pair * 8, 8), 8), :]
-             for jj in range(HALF_X_CHUNKS) for src in range(ny)]
-    first, second = swap_rows(jnp.concatenate(tiles[::2], axis=0), jnp.concatenate(tiles[1::2], axis=0))
-    lines = [first.reshape(-1, LANES), second.reshape(-1, LANES)]
+        for i in range(kc):
+            xi_wait(jj, i)
+
+
+def x_inverse(ebuf, wx, p, group, ny, crow, xrow):
+    def tile(jj, src, i):
+        at = (p * HALF_X_CHUNKS + jj) * crow + src * xrow + i * (xrow // 2) + group * 8
+        return ebuf[pl.ds(pl.multiple_of(at, 8), 8), :]
+
+    quads = [jnp.concatenate([tile(jj, src + k // 2, k % 2) for jj in range(HALF_X_CHUNKS) for src in range(0, ny, 2)], axis=0)
+             for k in range(4)]
+    a0, a2 = swap_rows(quads[0], quads[2])
+    a1, a3 = swap_rows(quads[1], quads[3])
+    lines = [v.reshape(-1, LANES) for v in (*swap_pairs(a0, a1), *swap_pairs(a2, a3))]
     return dot(jnp.concatenate(lines, axis=1), wx[p], ((0,), (0,)))
 
 
 def finish(ny, n, nf, ebuf, even, hat_re, hat_im, wx, phi_re, phi_im, out_re, out_im, stage, p_sem, h_sem):
     half = n // 2
     yl = n // ny
-    nj, pairs = 2 * HALF_X_CHUNKS, yl // 2
+    nj = 2 * HALF_X_CHUNKS
     crow = ebuf.shape[0] // nj
     xrow = crow // ny
     zl = phi_re.shape[2]
@@ -333,34 +348,31 @@
     for h in hats:
         h.start()
 
-    def phi_copy(c, pair):
-        slot = lax.rem(pair, OUT_SLOTS)
-        return pltpu.make_async_copy(stage.at[slot, c], phi[c].at[:, pl.ds(2 * pair, 2)], p_sem.at[slot, c])
+    def phi_copy(c, group):
+        slot = lax.rem(group, OUT_SLOTS)
+        return pltpu.make_async_copy(stage.at[slot, c], phi[c].at[:, pl.ds(4 * group, 4)], p_sem.at[slot, c])
 
     def body(group, carry):
-        @pl.when(group * GROUP >= OUT_SLOTS)
-        def _():
-            for u in range(GROUP):
-                for c in range(2):
-                    phi_copy(c, group * GROUP + u - OUT_SLOTS).wait()
-
-        for u in range(GROUP):
-            pair = group * GROUP + u
-            slot = lax.rem(pair, OUT_SLOTS)
-            e, o = even[pair], x_inverse(ebuf, wx, 1, pair, ny, crow, xrow)
-            for c in range(2):
-                ec, oc = e[:, c * half:(c + 1) * half], o[:, c * half:(c + 1) * half]
-                out = jnp.concatenate([ec + oc, ec - oc], axis=1).reshape(2, nf, zl, n)
-                stage[slot, c] = jnp.swapaxes(out, 0, 1)
-        for u in range(GROUP):
-            for c in range(2):
-                phi_copy(c, group * GROUP + u).start()
+        @pl.when(group >= OUT_SLOTS)
+        def _():
+            for c in range(2):
+                phi_copy(c, group - OUT_SLOTS).wait()
+
+        slot = lax.rem(group, OUT_SLOTS)
+        e, o = even[group], x_inverse(ebuf, wx, 1, group, ny, crow, xrow)
+        for c in range(2):
+            ec, oc = e[:, c * half:(c + 1) * half], o[:, c * half:(c + 1) * half]
+            out = jnp.concatenate([ec + oc, ec - oc], axis=1).reshape(4, nf, zl, n)
+            stage[slot, c] = jnp.swapaxes(out, 0, 1)
+        for c in range(2):
+            phi_copy(c, group).start()
         return carry
 
-    lax.fori_loop(0, pairs // GROUP, body, 0)
-    for pair in range(pairs - OUT_SLOTS, pairs):
+    groups = yl // 4
+    lax.fori_loop(0, groups, body, 0)
+    for group in range(groups - OUT_SLOTS, groups):
         for c in range(2):
-            phi_copy(c, pair).wait()
+            phi_copy(c, group).wait()
     for h in hats:
         h.wait()
 
@@ -384,7 +396,7 @@
         hbm = pl.BlockSpec(memory_space=pl.ANY)
         inner = pl.pallas_call(
             functools.partial(kernel, ny, nz, n, nf),
-            out_shape=(pltpu.VMEM((rows, LANES), jnp.float32), pltpu.VMEM((yl // 2, 2 * nf * zl, n), jnp.float32),
+            out_shape=(pltpu.VMEM((rows, LANES), jnp.float32), pltpu.VMEM((yl // 4, 4 * nf * zl, n), jnp.float32),
                        pltpu.VMEM(wave_shape, jnp.float32), pltpu.VMEM(wave_shape, jnp.float32)),
             in_specs=[hbm] * 8,
             out_specs=[vmem] * 4,
@@ -393,7 +405,7 @@
                 pltpu.VMEM((SLOTS, 2, nf, 2 * GROUP, zl, n), jnp.float32),
                 pltpu.VMEM((2, 2, kc, ml, n), jnp.float32),
                 *[pltpu.VMEM(t.shape, jnp.float32) for t in tables],
-                *[dma((nj,)) for _ in range(8)],
+                *[dma((nj,)) for _ in range(4)], *[dma((nj, kc)) for _ in range(4)],
                 dma((len(tables),)), dma((SLOTS, 2)), dma((2, 2)),
             ],
             compiler_params=pltpu.CompilerParams(
@@ -406,7 +418,7 @@
             out_shape=(space, space, wave, wave),
             in_specs=[vmem] * 5,
             out_specs=[hbm] * 4,
-            scratch_shapes=[pltpu.VMEM((OUT_SLOTS, 2, nf, 2, zl, n), jnp.float32), dma((OUT_SLOTS, 2)), dma((2,))],
+            scratch_shapes=[pltpu.VMEM((OUT_SLOTS, 2, nf, 4, zl, n), jnp.float32), dma((OUT_SLOTS, 2)), dma((2,))],
             compiler_params=pltpu.CompilerParams(vmem_limit_bytes=16 << 20),
             name="finish",
         )(*inner, tables[0])

time: 218 us -> 217 us (level)
  no operation moved by 1% of the time
where the time goes in v4:
time: 217 us
  Pallas kernels  216 us (100%)
    pallas_call x1, Pallas kernels, local_solve(): pl.pallas_call(functools.partial(kernel, ny, nz, n, nf), out_shape=(pltpu...  209 us
    pallas_call x1, Pallas kernels, local_solve(): pl.pallas_call(functools.partial(finish, ny, n, nf), out_shape=(space, sp...  7.36 us

profile of v4, /device:TPU:97, one launch (start us, length us, event | category | flops | bytes accessed | tf_op | source)
XLA Modules:
  0.0 216.9 jit_solution(5308539340882895473)
XLA Ops:
  0.6 0.0 copy-start
  0.6 208.9 %spectral.1 = (f32[16384,128]{1,0:T(8,128)S(1)}, f32[8,512,256]{2,1,0:T(8,128)S(1)}, f32[2,16,2,64,256]{4,3,2,1,0:T(8,128)S(1)}, f32[2,16,2,64,256]{4,3,2,1,0:T(8,128)S(1)}) custom-call(f32[2,32,64,256]{3,2,1,0:T(8,128)} %bitcast.8, f32[2,32,64,256]{3,2,1,0:T(8,128)} %bitcast.9, f32[16,2,64,256]{3,2,1,0:T(8,128)} %bitcast.10, f32[16,2,64,256]{3,2,1,0:T(8,128)} %bitcast.11, ...), custom_call_target="tpu_custom_call" | custom-call | tf_op jit(solution)/shard_map/spectral/pallas_call | solution.py:397
  209.5 0.0 copy-done
  209.5 7.4 %finish.1 = (f32[2,32,64,256]{3,2,1,0:T(8,128)}, f32[2,32,64,256]{3,2,1,0:T(8,128)}, f32[2,16,2,64,256]{4,3,2,1,0:T(8,128)}, f32[2,16,2,64,256]{4,3,2,1,0:T(8,128)}) custom-call(f32[16384,128]{1,0:T(8,128)S(1)} %get-tuple-element.12.ebuf, f32[8,512,256]{2,1,0:T(8,128)S(1)} %get-tuple-element.13.even, f32[2,16,2,64,256]{4,3,2,1,0:T(8,128)S(1)} %get-tuple-element.14.hat_re, ...), custom_call_target="tpu_custom_call" | custom-call | tf_op jit(solution)/shard_map/finish/pallas_call | solution.py:416
Async XLA Ops:
  0.6 208.9 %copy-start = (f32[2,256,256]{2,1,0:T(8,128)S(1)}, f32[2,256,256]{2,1,0:T(8,128)}, u32[]{:S(2)}) copy-start(f32[2,256,256]{2,1,0:T(8,128)} %constant.8.clone.wx_h.wx) | copy-start | bytes 1572868

commit v5 on v4

--- a/solution.py
+++ b/solution.py
@@ -13,6 +13,7 @@
 SLOTS = 3
 GROUP = 2
 OUT_SLOTS = 4
+DEPTH = 4
 LANES = 128
 INNER_VMEM = 42 << 20
 
@@ -70,7 +71,8 @@
     pairs = yl // 2
     groups = pairs // GROUP
     piece = groups // 4
-    sends = ((0, groups // 2), (groups // 2, piece), (groups - piece, piece // 2), (groups - piece // 2, piece // 2))
+    early, late, odd = range(HALF_X_CHUNKS // 2), range(HALF_X_CHUNKS // 2, HALF_X_CHUNKS), range(HALF_X_CHUNKS)
+    sends = [(k, 2) for k in range(0, groups - 2, 2)] + [(groups - 2, 1), (groups - 1, 1)]
     rho, gg, hat = (rho_re, rho_im), (g_re, g_im), (hat_re, hat_im)
     x_offsets = (4, 3, 5, 2, 6, 1, 7) if ny == 8 else tuple(range(1, ny))
     y_offsets = (2, 1, 3) if nz == 4 else tuple(range(1, nz))
@@ -88,25 +90,27 @@
         p, jj, slot = j // HALF_X_CHUNKS, lax.rem(j, HALF_X_CHUNKS), lax.rem(j, 2)
         return pltpu.make_async_copy(gg[c].at[pl.ds(kc * jj, kc), p], gbuf.at[slot, c], g_sem.at[slot, c])
 
-    def x_copy(src, dst, ss, rs, j, o, first=0, count=None, *half_of):
+    def x_copy(src, dst, ss, rs, j, o, first=0, count=None, sem=None):
         to = lax.rem(py + o, ny)
         rows = xrow if count is None else count
         return pltpu.make_async_remote_copy(
             src.at[pl.ds(pl.multiple_of(j * crow + to * xrow + first, 8), rows)],
             dst.at[pl.ds(pl.multiple_of(j * crow + py * xrow + first, 8), rows)],
-            ss.at[j, *half_of], rs.at[j, *half_of], device_id={"py": to}, device_id_type=MESH)
+            ss.at[j if sem is None else sem], rs.at[j if sem is None else sem],
+            device_id={"py": to}, device_id_type=MESH)
 
     def y_copy(src, dst, ss, rs, j, o, first=0, count=None, *half_of):
+        sem = (lax.rem(j, ys.shape[0]), *half_of)
         to = lax.rem(pz + o, nz)
         rows = yrow if count is None else count
         return pltpu.make_async_remote_copy(
             src.at[pl.ds(pl.multiple_of(j * crow + to * yrow + first, 8), rows)],
             dst.at[pl.ds(pl.multiple_of(j * crow + pz * yrow + first, 8), rows)],
-            ss.at[j, *half_of], rs.at[j, *half_of], device_id={"pz": to}, device_id_type=MESH)
+            ss.at[*sem], rs.at[*sem], device_id={"pz": to}, device_id_type=MESH)
 
     def await_all(src, dst, ss, rs, axis, me, size, rows, *of):
         at = pl.ds(pl.multiple_of(of[0] * crow, 8), rows)
-        pltpu.make_async_remote_copy(src.at[at], dst.at[at], ss.at[*of], rs.at[*of],
+        pltpu.make_async_remote_copy(src.at[at], dst.at[at], ss.at[lax.rem(of[0], ss.shape[0]), *of[1:]], rs.at[lax.rem(of[0], ss.shape[0]), *of[1:]],
                                      device_id={axis: lax.rem(me + 1, size)}, device_id_type=MESH).wait()
 
     def own(src, dst, j, mine, rows):
@@ -120,14 +124,17 @@
     xf_wait = functools.partial(await_all, abuf, bbuf, xs, xr, "py", py, ny, (ny - 1) * xrow)
     yf_wait = functools.partial(await_all, abuf, cbuf, ys, yr, "pz", pz, nz, (nz - 1) * yrow)
     yi_wait = functools.partial(await_all, cbuf, dbuf, yis, yir, "pz", pz, nz, (nz - 1) * yrow // 2)
-    xi_wait = functools.partial(await_all, bbuf, ebuf, xis, xir, "py", py, ny, (ny - 1) * xrow // 2)
+    def xi_wait(p):
+        at = pl.ds(p * HALF_X_CHUNKS * crow, HALF_X_CHUNKS * (ny - 1) * xrow)
+        pltpu.make_async_remote_copy(bbuf.at[at], ebuf.at[at], xis.at[p], xir.at[p],
+                                     device_id={"py": lax.rem(py + 1, ny)}, device_id_type=MESH).wait()
 
     def x_prefetch(first):
         for k in range(SLOTS - 1):
             for c in range(2):
                 rho_copy(c, first + k).start()
 
-    def x_forward(p, first, stop):
+    def x_forward(p, jjs, first, stop):
         def body(group, carry):
             @pl.when(group + SLOTS - 1 < stop)
             def _():
@@ -143,16 +150,17 @@
                 low, high = lines[..., :half], lines[..., half:]
                 both = low - high if p else low + high
                 folded.append(jnp.swapaxes(both, 0, 1).reshape(2 * GROUP * nf * zl, half))
-            out = dot(wx[p], jnp.concatenate(folded, axis=1), ((1,), (1,)))
+            per_jj = ny * 2 * kc
+            out = dot(wx[p, jjs[0] * per_jj:(jjs[-1] + 1) * per_jj], jnp.concatenate(folded, axis=1), ((1,), (1,)))
             for u in range(GROUP):
                 blocks = swap_rows(out[:, 2 * u * LANES:(2 * u + 1) * LANES],
                                    out[:, (2 * u + 1) * LANES:(2 * u + 2) * LANES])
-                for jj in range(HALF_X_CHUNKS):
+                for jj in jjs:
                     for to in range(ny):
-                        r = jj * ny + to
+                        r = (jj - jjs[0]) * ny + to
                         at = (p * HALF_X_CHUNKS + jj) * crow + to * xrow + (group * GROUP + u) * 8
                         abuf[pl.ds(pl.multiple_of(at, 8), 8), :] = blocks[r % 2][r // 2]
-            if p == 0:
+            if p == 0 and jjs[0] == 0:
                 for start, count in sends:
                     @pl.when(group == start + count - 1)
                     def _():
@@ -234,14 +242,14 @@
     for o in range(1, nz):
         pl.semaphore_signal(barrier, inc=1, device_id={"pz": lax.rem(pz + o, nz)}, device_id_type=MESH)
     tables[0].wait()
-    x_forward(0, 0, groups)
+    x_forward(0, early, 0, groups)
     for c in range(2):
         g_copy(c, 0).start()
         g_copy(c, 1).start()
     for table in tables[1:]:
         table.start()
     x_prefetch(0)
-    for jj in range(1, HALF_X_CHUNKS):
+    for jj in early[1:]:
         for o in x_offsets:
             xf(jj, o).start()
     for table in tables[1:]:
@@ -280,31 +288,38 @@
                 yi_wait(j, i)
                 y_inverse(j, i)
                 for o in x_offsets:
-                    xi(j, o, 2 * i * yl, 2 * yl, i).start()
+                    xi(j, o, 2 * i * yl, 2 * yl, j // HALF_X_CHUNKS).start()
             own(bbuf, ebuf, j, py, xrow)
 
-        @pl.when(t < 4)
-        def _():
-            x_forward(1, t * piece, (t + 1) * piece)
-
-            @pl.when(t < 3)
+        def spare(p, jjs, begin):
+            part = groups // 2
+
+            def send(j, c):
+                for o in x_offsets:
+                    xf(j, o).start()
+                return c
+
+            @pl.when((t >= begin) & (t < begin + 2))
             def _():
-                x_prefetch((t + 1) * piece)
-
-        @pl.when(t == 3)
-        def _():
-            def send(jj, c):
-                for o in x_offsets:
-                    xf(jj, o).start()
-                return c
-
-            lax.fori_loop(HALF_X_CHUNKS, nj, send, 0)
+                x_forward(p, jjs, (t - begin) * part, (t - begin + 1) * part)
+                if p == 0:
+                    x_prefetch(jnp.where(t == begin, part, 0))
+                else:
+                    @pl.when(t == begin)
+                    def _():
+                        x_prefetch(part)
+
+            @pl.when(t == begin + 1)
+            def _():
+                base = p * HALF_X_CHUNKS
+                lax.fori_loop(base + jjs[0], base + jjs[-1] + 1, send, 0)
+
+        spare(0, late, 0)
+        spare(1, odd, 2)
 
         @pl.when(t == nj - 4)
         def _():
-            for jj in range(HALF_X_CHUNKS):
-                for i in range(kc):
-                    xi_wait(jj, i)
+            xi_wait(0)
 
         @pl.when((t >= nj - 4) & (t < nj))
         def _():
@@ -318,9 +333,7 @@
         return carry
 
     lax.fori_loop(0, nj + 2, step, 0)
-    for jj in range(HALF_X_CHUNKS, nj):
-        for i in range(kc):
-            xi_wait(jj, i)
+    xi_wait(1)
 
 
 def x_inverse(ebuf, wx, p, group, ny, crow, xrow):
@@ -405,7 +418,8 @@
                 pltpu.VMEM((SLOTS, 2, nf, 2 * GROUP, zl, n), jnp.float32),
                 pltpu.VMEM((2, 2, kc, ml, n), jnp.float32),
                 *[pltpu.VMEM(t.shape, jnp.float32) for t in tables],
-                *[dma((nj,)) for _ in range(4)], *[dma((nj, kc)) for _ in range(4)],
+                dma((nj,)), dma((nj,)), dma((DEPTH,)), dma((DEPTH,)),
+                dma((DEPTH, kc)), dma((DEPTH, kc)), dma((2,)), dma((2,)),
                 dma((len(tables),)), dma((SLOTS, 2)), dma((2, 2)),
             ],
             compiler_params=pltpu.CompilerParams(

time: 217 us -> 215 us (level)
    pallas_call x1, Pallas kernels: 209 us -> 206 us  [local_solve(): pl.pallas_call(functools.partial(kernel, ny, nz, n, nf), out_shape=(pltpu...]
where the time goes in v5:
time: 215 us; the launch traced here: 214 us
  Pallas kernels  214 us (100%)
    pallas_call x1, Pallas kernels, local_solve(): pl.pallas_call(functools.partial(kernel, ny, nz, n, nf), out_shape=(pltpu...  206 us
    pallas_call x1, Pallas kernels, local_solve(): pl.pallas_call(functools.partial(finish, ny, n, nf), out_shape=(space, sp...  7.36 us

profile of v5, /device:TPU:97, one launch (start us, length us, event | category | flops | bytes accessed | tf_op | source)
XLA Modules:
  0.0 214.5 jit_solution(14961117601241170689)
XLA Ops:
  0.6 0.0 copy-start
  0.6 206.5 %spectral.1 = (f32[16384,128]{1,0:T(8,128)S(1)}, f32[8,512,256]{2,1,0:T(8,128)S(1)}, f32[2,16,2,64,256]{4,3,2,1,0:T(8,128)S(1)}, f32[2,16,2,64,256]{4,3,2,1,0:T(8,128)S(1)}) custom-call(f32[2,32,64,256]{3,2,1,0:T(8,128)} %bitcast.8, f32[2,32,64,256]{3,2,1,0:T(8,128)} %bitcast.9, f32[16,2,64,256]{3,2,1,0:T(8,128)} %bitcast.10, f32[16,2,64,256]{3,2,1,0:T(8,128)} %bitcast.11, ...), custom_call_target="tpu_custom_call" | custom-call | tf_op jit(solution)/shard_map/spectral/pallas_call | solution.py:410
  207.1 0.0 copy-done
  207.1 7.4 %finish.1 = (f32[2,32,64,256]{3,2,1,0:T(8,128)}, f32[2,32,64,256]{3,2,1,0:T(8,128)}, f32[2,16,2,64,256]{4,3,2,1,0:T(8,128)}, f32[2,16,2,64,256]{4,3,2,1,0:T(8,128)}) custom-call(f32[16384,128]{1,0:T(8,128)S(1)} %get-tuple-element.12.ebuf, f32[8,512,256]{2,1,0:T(8,128)S(1)} %get-tuple-element.13.even, f32[2,16,2,64,256]{4,3,2,1,0:T(8,128)S(1)} %get-tuple-element.14.hat_re, ...), custom_call_target="tpu_custom_call" | custom-call | tf_op jit(solution)/shard_map/finish/pallas_call | solution.py:430
Async XLA Ops:
  0.6 206.5 %copy-start = (f32[2,256,256]{2,1,0:T(8,128)S(1)}, f32[2,256,256]{2,1,0:T(8,128)}, u32[]{:S(2)}) copy-start(f32[2,256,256]{2,1,0:T(8,128)} %constant.8.clone.wx_h.wx) | copy-start | bytes 1572868

commit v6 on v5

--- a/solution.py
+++ b/solution.py
@@ -12,10 +12,12 @@
 HALF_X_CHUNKS = 8
 SLOTS = 3
 GROUP = 2
-OUT_SLOTS = 4
+OUT_SLOTS = 6
+REFINE_EARLY = 3
 DEPTH = 4
+SPLIT = 4
 LANES = 128
-INNER_VMEM = 42 << 20
+INNER_VMEM = 35 << 20
 
 
 def real_form(matrix):
@@ -58,8 +60,8 @@
 
 def kernel(ny, nz, n, nf,
            rho_re, rho_im, g_re, g_im, wx_h, wy_h, wz_h, wyi_h,
-           ebuf, even, hat_re, hat_im,
-           abuf, bbuf, cbuf, dbuf, stage, gbuf, wx, wy, wz, wyi,
+           ebuf, abuf, hat_re, hat_im,
+           bbuf, cbuf, dbuf, stage, gbuf, wx, wy, wz, wyi,
            xs, xr, ys, yr, yis, yir, xis, xir, w_sem, in_sem, g_sem):
     py, pz = lax.axis_index("py"), lax.axis_index("pz")
     half = n // 2
@@ -124,9 +126,11 @@
     xf_wait = functools.partial(await_all, abuf, bbuf, xs, xr, "py", py, ny, (ny - 1) * xrow)
     yf_wait = functools.partial(await_all, abuf, cbuf, ys, yr, "pz", pz, nz, (nz - 1) * yrow)
     yi_wait = functools.partial(await_all, cbuf, dbuf, yis, yir, "pz", pz, nz, (nz - 1) * yrow // 2)
-    def xi_wait(p):
-        at = pl.ds(p * HALF_X_CHUNKS * crow, HALF_X_CHUNKS * (ny - 1) * xrow)
-        pltpu.make_async_remote_copy(bbuf.at[at], ebuf.at[at], xis.at[p], xir.at[p],
+    cuts = (0, HALF_X_CHUNKS, HALF_X_CHUNKS + SPLIT, nj)
+
+    def xi_wait(k):
+        at = pl.ds(cuts[k] * crow, (cuts[k + 1] - cuts[k]) * (ny - 1) * xrow)
+        pltpu.make_async_remote_copy(bbuf.at[at], ebuf.at[at], xis.at[k], xir.at[k],
                                      device_id={"py": lax.rem(py + 1, ny)}, device_id_type=MESH).wait()
 
     def x_prefetch(first):
@@ -235,8 +239,11 @@
                     at = base + (s * (ny // 2) + to) * xrow + 2 * i * yl + c
                     bbuf[pl.ds(at, yl, stride=2), :] = out[c * half + to * yl:c * half + (to + 1) * yl]
 
-    x_prefetch(0)
+    for c in range(2):
+        rho_copy(c, 0).start()
     tables[0].start()
+    for c in range(2):
+        rho_copy(c, 1).start()
     for o in range(1, ny):
         pl.semaphore_signal(barrier, inc=1, device_id={"py": lax.rem(py + o, ny)}, device_id_type=MESH)
     for o in range(1, nz):
@@ -288,7 +295,7 @@
                 yi_wait(j, i)
                 y_inverse(j, i)
                 for o in x_offsets:
-                    xi(j, o, 2 * i * yl, 2 * yl, j // HALF_X_CHUNKS).start()
+                    xi(j, o, 2 * i * yl, 2 * yl, jnp.where(j < cuts[1], 0, jnp.where(j < cuts[2], 1, 2))).start()
             own(bbuf, ebuf, j, py, xrow)
 
         def spare(p, jjs, begin):
@@ -323,33 +330,54 @@
 
         @pl.when((t >= nj - 4) & (t < nj))
         def _():
-            def body(k, c):
-                group = (t - (nj - 4)) * piece + k
-                even[group] = x_inverse(ebuf, wx, 0, group, ny, crow, xrow)
+            def body(group, c):
+                e = x_inverse(ebuf, wx, 0, odd, group, ny, crow, xrow)
+                for c2 in range(2):
+                    abuf[part_rows(0, group, c2, crow), :] = e[:, c2 * half:(c2 + 1) * half]
                 return c
 
-            lax.fori_loop(0, piece, body, 0)
+            first = (t - (nj - 4)) * piece
+            lax.fori_loop(first, first + piece, body, 0)
+
+        @pl.when(t == nj - 1)
+        def _():
+            xi_wait(1)
+            lax.fori_loop(0, REFINE_EARLY, refine, 0)
 
         return carry
 
+    def refine(group, carry):
+        o = x_inverse(ebuf, wx, 1, range(SPLIT), group, ny, crow, xrow)
+        for c in range(2):
+            e, oc = abuf[part_rows(0, group, c, crow), :], o[:, c * half:(c + 1) * half]
+            abuf[part_rows(0, group, c, crow), :] = e + oc
+            abuf[part_rows(1, group, c, crow), :] = e - oc
+        return carry
+
     lax.fori_loop(0, nj + 2, step, 0)
-    xi_wait(1)
-
-
-def x_inverse(ebuf, wx, p, group, ny, crow, xrow):
+    lax.fori_loop(REFINE_EARLY, groups, refine, 0)
+    xi_wait(2)
+
+
+def part_rows(sign, group, c, crow):
+    return pl.ds(pl.multiple_of((sign * HALF_X_CHUNKS + group) * crow + c * (crow // 2), 8), crow // 2)
+
+
+def x_inverse(ebuf, wx, p, jjs, group, ny, crow, xrow):
     def tile(jj, src, i):
         at = (p * HALF_X_CHUNKS + jj) * crow + src * xrow + i * (xrow // 2) + group * 8
         return ebuf[pl.ds(pl.multiple_of(at, 8), 8), :]
 
-    quads = [jnp.concatenate([tile(jj, src + k // 2, k % 2) for jj in range(HALF_X_CHUNKS) for src in range(0, ny, 2)], axis=0)
+    quads = [jnp.concatenate([tile(jj, src + k // 2, k % 2) for jj in jjs for src in range(0, ny, 2)], axis=0)
              for k in range(4)]
     a0, a2 = swap_rows(quads[0], quads[2])
     a1, a3 = swap_rows(quads[1], quads[3])
     lines = [v.reshape(-1, LANES) for v in (*swap_pairs(a0, a1), *swap_pairs(a2, a3))]
-    return dot(jnp.concatenate(lines, axis=1), wx[p], ((0,), (0,)))
-
-
-def finish(ny, n, nf, ebuf, even, hat_re, hat_im, wx, phi_re, phi_im, out_re, out_im, stage, p_sem, h_sem):
+    per_jj = 4 * ny
+    return dot(jnp.concatenate(lines, axis=1), wx[p, jjs[0] * per_jj:(jjs[-1] + 1) * per_jj], ((0,), (0,)))
+
+
+def finish(ny, n, nf, ebuf, abuf, hat_re, hat_im, wx, phi_re, phi_im, out_re, out_im, stage, p_sem, h_sem):
     half = n // 2
     yl = n // ny
     nj = 2 * HALF_X_CHUNKS
@@ -372,10 +400,11 @@
                 phi_copy(c, group - OUT_SLOTS).wait()
 
         slot = lax.rem(group, OUT_SLOTS)
-        e, o = even[group], x_inverse(ebuf, wx, 1, group, ny, crow, xrow)
+        o = x_inverse(ebuf, wx, 1, range(SPLIT, HALF_X_CHUNKS), group, ny, crow, xrow)
         for c in range(2):
-            ec, oc = e[:, c * half:(c + 1) * half], o[:, c * half:(c + 1) * half]
-            out = jnp.concatenate([ec + oc, ec - oc], axis=1).reshape(4, nf, zl, n)
+            low, high = (abuf[part_rows(sign, group, c, crow), :] for sign in range(2))
+            oc = o[:, c * half:(c + 1) * half]
+            out = jnp.concatenate([low + oc, high - oc], axis=1).reshape(4, nf, zl, n)
             stage[slot, c] = jnp.swapaxes(out, 0, 1)
         for c in range(2):
             phi_copy(c, group).start()
@@ -409,17 +438,17 @@
         hbm = pl.BlockSpec(memory_space=pl.ANY)
         inner = pl.pallas_call(
             functools.partial(kernel, ny, nz, n, nf),
-            out_shape=(pltpu.VMEM((rows, LANES), jnp.float32), pltpu.VMEM((yl // 4, 4 * nf * zl, n), jnp.float32),
+            out_shape=(pltpu.VMEM((rows, LANES), jnp.float32), pltpu.VMEM((rows, LANES), jnp.float32),
                        pltpu.VMEM(wave_shape, jnp.float32), pltpu.VMEM(wave_shape, jnp.float32)),
             in_specs=[hbm] * 8,
             out_specs=[vmem] * 4,
             scratch_shapes=[
-                buf, buf, buf, buf,
+                buf, buf, buf,
                 pltpu.VMEM((SLOTS, 2, nf, 2 * GROUP, zl, n), jnp.float32),
                 pltpu.VMEM((2, 2, kc, ml, n), jnp.float32),
                 *[pltpu.VMEM(t.shape, jnp.float32) for t in tables],
                 dma((nj,)), dma((nj,)), dma((DEPTH,)), dma((DEPTH,)),
-                dma((DEPTH, kc)), dma((DEPTH, kc)), dma((2,)), dma((2,)),
+                dma((DEPTH, kc)), dma((DEPTH, kc)), dma((3,)), dma((3,)),
                 dma((len(tables),)), dma((SLOTS, 2)), dma((2, 2)),
             ],
             compiler_params=pltpu.CompilerParams(
@@ -433,7 +462,7 @@
             in_specs=[vmem] * 5,
             out_specs=[hbm] * 4,
             scratch_shapes=[pltpu.VMEM((OUT_SLOTS, 2, nf, 4, zl, n), jnp.float32), dma((OUT_SLOTS, 2)), dma((2,))],
-            compiler_params=pltpu.CompilerParams(vmem_limit_bytes=16 << 20),
+            compiler_params=pltpu.CompilerParams(vmem_limit_bytes=8 << 20),
             name="finish",
         )(*inner, tables[0])
         phi = [jnp.transpose(v, (0, 3, 1, 2)) for v in outs[:2]]

time: 215 us -> 214 us (level)
  no operation moved by 1% of the time
where the time goes in v6:
time: 214 us; the launch traced here: 213 us
  Pallas kernels  213 us (100%)
    pallas_call x1, Pallas kernels, local_solve(): pl.pallas_call(functools.partial(kernel, ny, nz, n, nf), out_shape=(pltpu...  206 us
    pallas_call x1, Pallas kernels, local_solve(): pl.pallas_call(functools.partial(finish, ny, n, nf), out_shape=(space, sp...  6.31 us

profile of v6, /device:TPU:97, one launch (start us, length us, event | category | flops | bytes accessed | tf_op | source)
XLA Modules:
  0.0 213.3 jit_solution(3700746398564158204)
XLA Ops:
  0.6 0.0 copy-start
  0.6 206.4 %spectral.1 = (f32[16384,128]{1,0:T(8,128)S(1)}, f32[16384,128]{1,0:T(8,128)S(1)}, f32[2,16,2,64,256]{4,3,2,1,0:T(8,128)S(1)}, f32[2,16,2,64,256]{4,3,2,1,0:T(8,128)S(1)}) custom-call(f32[2,32,64,256]{3,2,1,0:T(8,128)} %bitcast.8, f32[2,32,64,256]{3,2,1,0:T(8,128)} %bitcast.9, f32[16,2,64,256]{3,2,1,0:T(8,128)} %bitcast.10, f32[16,2,64,256]{3,2,1,0:T(8,128)} %bitcast.11, ...), custom_call_target="tpu_custom_call" | custom-call | tf_op jit(solution)/shard_map/spectral/pallas_call | solution.py:439
  207.0 0.0 copy-done
  207.0 6.3 %finish.1 = (f32[2,32,64,256]{3,2,1,0:T(8,128)}, f32[2,32,64,256]{3,2,1,0:T(8,128)}, f32[2,16,2,64,256]{4,3,2,1,0:T(8,128)}, f32[2,16,2,64,256]{4,3,2,1,0:T(8,128)}) custom-call(f32[16384,128]{1,0:T(8,128)S(1)} %get-tuple-element.12.ebuf, f32[16384,128]{1,0:T(8,128)S(1)} %get-tuple-element.13.abuf, f32[2,16,2,64,256]{4,3,2,1,0:T(8,128)S(1)} %get-tuple-element.14.hat_re, ...), custom_call_target="tpu_custom_call" | custom-call | tf_op jit(solution)/shard_map/finish/pallas_call | solution.py:459
Async XLA Ops:
  0.6 206.4 %copy-start = (f32[2,256,256]{2,1,0:T(8,128)S(1)}, f32[2,256,256]{2,1,0:T(8,128)}, u32[]{:S(2)}) copy-start(f32[2,256,256]{2,1,0:T(8,128)} %constant.8.clone.wx_h.wx) | copy-start | bytes 1572868
